TPU v7x, 32 devices: a whole 2x2x4 slice. The times are simulated.
32 devices in a mesh: dp: 8 (over z, core), tensor: 4 (over y, x).
Axes of the slice: x: 2, y: 2, z: 4, core: 2. Of those that a mesh axis runs over, the one named last changes fastest.
Arguments:
- streams: bfloat16 [4, 20480, 2048], P(None, ('dp', 'tensor')), may hold values from -6 to 6
- prior: bfloat16 [3, 20480, 2048], P(None, ('dp', 'tensor')), may hold values from -6 to 6
- seg_ids: int32 [20480], P('dp'), may hold values from 0 to 2, as said below
- positions: int32 [20480], P('dp'), may hold values from 0 to 2558, as said below
- w_qk: bfloat16 [2, 2048, 2048], P(None, 'dp', 'tensor'), may hold values from -0.1875 to 0.1875
- w_value: bfloat16 [2048, 2048], P('dp', 'tensor'), may hold values from -0.125 to 0.125
- w_out: bfloat16 [2048, 2048], P('tensor', 'dp'), may hold values from -0.5 to 0.5
- w_up: bfloat16 [2048, 8192], P('dp', 'tensor'), may hold values from -0.125 to 0.125
- w_down: bfloat16 [8192, 2048], P('tensor', 'dp'), may hold values from -0.0625 to 0.0625
- norm_gain: bfloat16 [5, 2048], P(None, 'dp'), may hold values from 0.099609375 to 1.8984375
- norm_bias: bfloat16 [5, 2048], P(None, 'dp'), may hold values from -3 to 3
- mix_in: bfloat16 [2048, 16], P('dp'), may hold values from -0.125 to 0.125
- mix_out: bfloat16 [16, 16], P(None, 'dp'), may hold values from -1.5 to 1.5
- mix_bias: bfloat16 [16], P('dp'), may hold values from -3 to 3
- d_streams: bfloat16 [4, 20480, 2048], P(None, ('dp', 'tensor')), may hold values from -6 to 6
Outputs:
- new_streams: bfloat16 [4, 20480, 2048], P(None, ('dp', 'tensor'))
- grad_streams: bfloat16 [4, 20480, 2048], P(None, ('dp', 'tensor'))
- grad_prior: bfloat16 [3, 20480, 2048], P(None, ('dp', 'tensor'))
- grad_w_qk: float32 [2, 2048, 2048], P(None, 'dp', 'tensor')
- grad_w_value: float32 [2048, 2048], P('dp', 'tensor')
- grad_w_out: float32 [2048, 2048], P('tensor', 'dp')
- grad_w_up: float32 [2048, 8192], P('dp', 'tensor')
- grad_w_down: float32 [8192, 2048], P('tensor', 'dp')
- grad_norm_gain: float32 [5, 2048], P(None, 'dp')
- grad_norm_bias: float32 [5, 2048], P(None, 'dp')
- grad_mix_in: float32 [2048, 16], P('dp')
- grad_mix_out: float32 [16, 16], P(None, 'dp')
- grad_mix_bias: float32 [16], P('dp')
Inputs may be any that keep to these rules, and one draw needn't show every extreme that they name: `seg_ids`: each group of 2560 consecutive tokens holds 2048 prompt tokens of segment 0 followed by 2 continuations of 256 tokens; every token of a continuation carries that continuation's segment, a number of 1 to 2; several continuations of a group may carry the same segment, and the first continuation of every group carries 2. Prompt tokens have positions 0 to 2047 in order; a continuation's positions rise by one from a start between 2048 and 2303, and the first continuation of every group starts at the latest.
All inputs are finite; a program needn't handle non-finite values.
Results may differ from a plain program's by a relative error of at most 0.02.
Values may be sent and summed in bfloat16 or wider, within the bound.
A program may use at most 512 MiB of HBM per device.

v0:
```python
import math

import jax
import jax.numpy as jnp
from jax import lax
from jax.sharding import PartitionSpec as P

HDIM = 128


EPSILON = 1e-05
MASKED_SCORE = -1e30
HIGHEST_PRECISION = lax.Precision.HIGHEST


def layer_norm(inputs, gain_row, shift_row):
    centre = inputs - jnp.mean(inputs, axis=-1, keepdims=True)
    spread = jnp.mean(centre * centre, axis=-1, keepdims=True)
    return centre * lax.rsqrt(spread + EPSILON) * gain_row + shift_row


def norm_back(inputs, gain_row, shift_row, upstream):
    unused_value, pull_back = jax.vjp(layer_norm, inputs, gain_row, shift_row)
    return pull_back(upstream)


def gelu_exact(inputs):
    return jax.nn.gelu(inputs, approximate=False)


def rotary_tables(position_row, head_width):
    half_width = head_width // 2
    frequency = jnp.exp(
        jnp.arange(half_width, dtype=jnp.float32) * (-2.0 * math.log(10000.0) / head_width)
    )
    angles = position_row.astype(jnp.float32)[:, None] * frequency[None, :]
    return (jnp.cos(angles)[:, None, :], jnp.sin(angles)[:, None, :])


def rotate(inputs, cosine_table, sine_table):
    half_width = inputs.shape[-1] // 2
    first_half = inputs[..., :half_width]
    second_half = inputs[..., half_width:]
    return jnp.concatenate(
        [
            first_half * cosine_table - second_half * sine_table,
            second_half * cosine_table + first_half * sine_table,
        ],
        axis=-1,
    )


def visible(segment_query, position_query, segment_keys, position_keys):
    shared = (segment_keys[None, :] == 0) | (segment_keys[None, :] == segment_query[:, None])
    return shared & (position_keys[None, :] <= position_query[:, None])


def contract_first(left, right):
    return lax.dot_general(
        left, right, (((0,), (0,)), ((), ())), preferred_element_type=jnp.float32
    )


def contract_last(left, right):
    return lax.dot_general(
        left, right, (((1,), (1,)), ((), ())), preferred_element_type=jnp.float32
    )


def body(
    streams,
    prior,
    seg_ids,
    positions,
    w_qk,
    w_value,
    w_out,
    w_up,
    w_down,
    norm_gain,
    norm_bias,
    mix_in,
    mix_out,
    mix_bias,
    d_streams,
):
    rows_dev = streams.shape[1]
    group_rows = rows_dev * lax.axis_size("tensor")
    block_rows = min(512, group_rows)
    block_count = group_rows // block_rows
    score_scale = 1.0 / math.sqrt(HDIM)
    (
        qk_all,
        value_all,
        out_all,
        up_all,
        down_all,
        gain_all,
        shift_all,
        mixin_all,
        mixout_all,
        mixbias_all,
    ) = (
        lax.all_gather(w_qk, "dp", axis=1, tiled=True),
        lax.all_gather(w_value, "dp", axis=0, tiled=True),
        lax.all_gather(w_out, "dp", axis=1, tiled=True),
        lax.all_gather(w_up, "dp", axis=0, tiled=True),
        lax.all_gather(w_down, "dp", axis=1, tiled=True),
        lax.all_gather(norm_gain, "dp", axis=1, tiled=True),
        lax.all_gather(norm_bias, "dp", axis=1, tiled=True),
        lax.all_gather(mix_in, "dp", axis=0, tiled=True),
        lax.all_gather(mix_out, "dp", axis=1, tiled=True),
        lax.all_gather(mix_bias, "dp", axis=0, tiled=True),
    )
    gains = gain_all.astype(jnp.float32)
    shifts = shift_all.astype(jnp.float32)
    inputs = streams.astype(jnp.float32)
    normed_q = layer_norm(inputs[0], gains[0], shifts[0]).astype(jnp.bfloat16)
    normed_k = layer_norm(inputs[1], gains[1], shifts[1]).astype(jnp.bfloat16)
    normed_v = layer_norm(inputs[2], gains[2], shifts[2]).astype(jnp.bfloat16)
    query_rows, key_rows, value_rows = (
        lax.all_gather(normed_q, "tensor", axis=0, tiled=True),
        lax.all_gather(normed_k, "tensor", axis=0, tiled=True),
        lax.all_gather(normed_v, "tensor", axis=0, tiled=True),
    )
    local_cols = value_all.shape[1]
    head_count = local_cols // HDIM
    cosine_table, sine_table = rotary_tables(positions, HDIM)
    query_rot = rotate(
        jnp.dot(query_rows, qk_all[0], preferred_element_type=jnp.float32).reshape(
            group_rows, head_count, HDIM
        ),
        cosine_table,
        sine_table,
    ).astype(jnp.bfloat16)
    key_rot = rotate(
        jnp.dot(key_rows, qk_all[1], preferred_element_type=jnp.float32).reshape(
            group_rows, head_count, HDIM
        ),
        cosine_table,
        sine_table,
    ).astype(jnp.bfloat16)
    value_heads = (
        jnp.dot(value_rows, value_all, preferred_element_type=jnp.float32)
        .astype(jnp.bfloat16)
        .reshape(group_rows, head_count, HDIM)
    )

    def block_scores(first_row):
        query_block = lax.dynamic_slice_in_dim(query_rot, first_row, block_rows)
        scores = (
            jnp.einsum("qhe,khe->hqk", query_block, key_rot, preferred_element_type=jnp.float32)
            * score_scale
        )
        pairs = visible(
            lax.dynamic_slice_in_dim(seg_ids, first_row, block_rows),
            lax.dynamic_slice_in_dim(positions, first_row, block_rows),
            seg_ids,
            positions,
        )
        return (jnp.where(pairs[None], scores, MASKED_SCORE), query_block)

    def forward_block(block_index):
        scores = block_scores(block_index * block_rows)[0]
        row_max = jnp.max(scores, axis=-1, keepdims=True)
        log_total = row_max + jnp.log(jnp.sum(jnp.exp(scores - row_max), axis=-1, keepdims=True))
        probs_low = jnp.exp(scores - log_total).astype(jnp.bfloat16)
        block_out = jnp.einsum(
            "hqk,khe->qhe", probs_low, value_heads, preferred_element_type=jnp.float32
        )
        return (block_out.astype(jnp.bfloat16), log_total)

    attended, log_totals = lax.map(forward_block, jnp.arange(block_count, dtype=jnp.int32))
    attended = attended.reshape(group_rows, local_cols)
    qk_full, value_full, out_full = (
        lax.all_gather(qk_all, "tensor", axis=2, tiled=True),
        lax.all_gather(value_all, "tensor", axis=1, tiled=True),
        lax.all_gather(out_all, "tensor", axis=0, tiled=True),
    )
    attended_rows = lax.all_to_all(attended, "tensor", split_axis=0, concat_axis=1, tiled=True)
    attn_result = jnp.dot(attended_rows, out_full, preferred_element_type=jnp.float32)
    mid_stream = inputs[3] + attn_result
    mlp_input = layer_norm(mid_stream, gains[3], shifts[3]).astype(jnp.bfloat16)
    mlp_rows = lax.all_gather(mlp_input, "tensor", axis=0, tiled=True)
    hidden_pre = jnp.dot(mlp_rows, up_all, preferred_element_type=jnp.float32)
    hidden = gelu_exact(hidden_pre).astype(jnp.bfloat16)
    mlp_result = lax.psum_scatter(
        jnp.dot(hidden, down_all, preferred_element_type=jnp.float32),
        "tensor",
        scatter_dimension=0,
        tiled=True,
    )
    layer_out = mid_stream + mlp_result
    mix_normed = layer_norm(layer_out, gains[4], shifts[4]).astype(jnp.bfloat16)
    mix_pre = jnp.dot(mix_normed, mixin_all, preferred_element_type=jnp.float32)
    mix_act = gelu_exact(mix_pre)
    mix_weight = mixout_all.astype(jnp.float32)
    mix_coef = jnp.dot(mix_act, mix_weight, precision=HIGHEST_PRECISION) + mixbias_all.astype(
        jnp.float32
    )
    sources = jnp.concatenate([prior.astype(jnp.float32), layer_out[None]], axis=0)
    source_count = sources.shape[0]
    coef_table = mix_coef.reshape(rows_dev, 4, source_count)
    mixed = jnp.einsum("rsj,jrd->srd", coef_table, sources, precision=HIGHEST_PRECISION)
    new_streams = mixed.astype(jnp.bfloat16)
    grad_output = d_streams.astype(jnp.float32)
    grad_coef = jnp.einsum(
        "srd,jrd->rsj", grad_output, sources, precision=HIGHEST_PRECISION
    ).reshape(rows_dev, 4 * source_count)
    grad_sources = jnp.einsum("rsj,srd->jrd", coef_table, grad_output, precision=HIGHEST_PRECISION)
    grad_prior = grad_sources[:-1].astype(jnp.bfloat16)
    grad_mix_bias = jnp.sum(grad_coef, axis=0)
    grad_mix_out = lax.dot_general(
        mix_act,
        grad_coef,
        (((0,), (0,)), ((), ())),
        precision=HIGHEST_PRECISION,
        preferred_element_type=jnp.float32,
    )
    grad_act = lax.dot_general(
        grad_coef,
        mix_weight,
        (((1,), (1,)), ((), ())),
        precision=HIGHEST_PRECISION,
        preferred_element_type=jnp.float32,
    )
    unused_mix, mix_pull = jax.vjp(gelu_exact, mix_pre)
    grad_pre = mix_pull(grad_act)[0].astype(jnp.bfloat16)
    grad_mix_in = contract_first(mix_normed, grad_pre)
    grad_normed = contract_last(grad_pre, mixin_all)
    grad_from_mix, gain_four, shift_four = norm_back(layer_out, gains[4], shifts[4], grad_normed)
    grad_layer = grad_sources[-1] + grad_from_mix
    grad_out_rows = lax.all_gather(grad_layer.astype(jnp.bfloat16), "tensor", axis=0, tiled=True)
    grad_w_down = contract_first(hidden, grad_out_rows)
    grad_hidden = contract_last(grad_out_rows, down_all)
    unused_hidden, hidden_pull = jax.vjp(gelu_exact, hidden_pre)
    grad_hidden_pre = hidden_pull(grad_hidden)[0].astype(jnp.bfloat16)
    grad_w_up = contract_first(mlp_rows, grad_hidden_pre)
    grad_mlp_input = lax.psum_scatter(
        contract_last(grad_hidden_pre, up_all).astype(jnp.bfloat16),
        "tensor",
        scatter_dimension=0,
        tiled=True,
    ).astype(jnp.float32)
    grad_from_mlp, gain_three, shift_three = norm_back(
        mid_stream, gains[3], shifts[3], grad_mlp_input
    )
    grad_mid = grad_layer + grad_from_mlp
    grad_attn_rows = lax.all_gather(grad_mid.astype(jnp.bfloat16), "tensor", axis=0, tiled=True)
    grad_w_out = contract_first(attended, grad_attn_rows)
    grad_attended = (
        contract_last(grad_attn_rows, out_all)
        .astype(jnp.bfloat16)
        .reshape(group_rows, head_count, HDIM)
    )

    def backward_block(running, block_index):
        grad_key_sum, grad_value_sum = running
        first_row = block_index * block_rows
        scores, query_block = block_scores(first_row)
        block_probs = jnp.exp(scores - log_totals[block_index])
        grad_block = lax.dynamic_slice_in_dim(grad_attended, first_row, block_rows)
        grad_probs = jnp.einsum(
            "qhe,khe->hqk", grad_block, value_heads, preferred_element_type=jnp.float32
        )
        row_inner = jnp.sum(block_probs * grad_probs, axis=-1, keepdims=True)
        grad_scores = (block_probs * (grad_probs - row_inner)).astype(jnp.bfloat16)
        grad_query_block = (
            jnp.einsum("hqk,khe->qhe", grad_scores, key_rot, preferred_element_type=jnp.float32)
            * score_scale
        )
        grad_key_sum = (
            grad_key_sum
            + jnp.einsum(
                "hqk,qhe->khe", grad_scores, query_block, preferred_element_type=jnp.float32
            )
            * score_scale
        )
        grad_value_sum = grad_value_sum + jnp.einsum(
            "hqk,qhe->khe",
            block_probs.astype(jnp.bfloat16),
            grad_block,
            preferred_element_type=jnp.float32,
        )
        return ((grad_key_sum, grad_value_sum), grad_query_block)

    zero_carry = jnp.zeros((group_rows, head_count, HDIM), jnp.float32)
    (grad_key_sum, grad_value_sum), grad_query_blocks = lax.scan(
        backward_block, (zero_carry, zero_carry), jnp.arange(block_count, dtype=jnp.int32)
    )
    grad_query_rot = grad_query_blocks.reshape(group_rows, head_count, HDIM)
    grad_query = (
        rotate(grad_query_rot, cosine_table, -sine_table)
        .astype(jnp.bfloat16)
        .reshape(group_rows, local_cols)
    )
    grad_key = (
        rotate(grad_key_sum, cosine_table, -sine_table)
        .astype(jnp.bfloat16)
        .reshape(group_rows, local_cols)
    )
    grad_value = grad_value_sum.astype(jnp.bfloat16).reshape(group_rows, local_cols)
    grad_w_qk = jnp.stack(
        [contract_first(query_rows, grad_query), contract_first(key_rows, grad_key)]
    )
    grad_w_value = contract_first(value_rows, grad_value)
    query_grad_rows, key_grad_rows, value_grad_rows = (
        lax.all_to_all(grad_query, "tensor", split_axis=0, concat_axis=1, tiled=True),
        lax.all_to_all(grad_key, "tensor", split_axis=0, concat_axis=1, tiled=True),
        lax.all_to_all(grad_value, "tensor", split_axis=0, concat_axis=1, tiled=True),
    )
    back_q = contract_last(query_grad_rows, qk_full[0])
    back_k = contract_last(key_grad_rows, qk_full[1])
    back_v = contract_last(value_grad_rows, value_full)
    grad_stream_q, gain_zero, shift_zero = norm_back(inputs[0], gains[0], shifts[0], back_q)
    grad_stream_k, gain_one, shift_one = norm_back(inputs[1], gains[1], shifts[1], back_k)
    grad_stream_v, gain_two, shift_two = norm_back(inputs[2], gains[2], shifts[2], back_v)
    grad_streams = jnp.stack([grad_stream_q, grad_stream_k, grad_stream_v, grad_mid]).astype(
        jnp.bfloat16
    )
    shard_qk, shard_value, shard_out, shard_up, shard_down = (
        lax.psum_scatter(
            grad_w_qk.astype(jnp.bfloat16), "dp", scatter_dimension=1, tiled=True
        ).astype(jnp.float32),
        lax.psum_scatter(
            grad_w_value.astype(jnp.bfloat16), "dp", scatter_dimension=0, tiled=True
        ).astype(jnp.float32),
        lax.psum_scatter(
            grad_w_out.astype(jnp.bfloat16), "dp", scatter_dimension=1, tiled=True
        ).astype(jnp.float32),
        lax.psum_scatter(
            grad_w_up.astype(jnp.bfloat16), "dp", scatter_dimension=0, tiled=True
        ).astype(jnp.float32),
        lax.psum_scatter(
            grad_w_down.astype(jnp.bfloat16), "dp", scatter_dimension=1, tiled=True
        ).astype(jnp.float32),
    )
    gain_parts = jnp.stack([gain_zero, gain_one, gain_two, gain_three, gain_four])
    shift_parts = jnp.stack([shift_zero, shift_one, shift_two, shift_three, shift_four])
    total_gain, total_shift, total_mix_in, total_mix_out, total_mix_bias = lax.psum(
        (gain_parts, shift_parts, grad_mix_in, grad_mix_out, grad_mix_bias), ("dp", "tensor")
    )
    dp_index = lax.axis_index("dp")
    norm_cols = norm_gain.shape[1]
    grad_norm_gain = lax.dynamic_slice_in_dim(total_gain, dp_index * norm_cols, norm_cols, 1)
    grad_norm_bias = lax.dynamic_slice_in_dim(total_shift, dp_index * norm_cols, norm_cols, 1)
    mixin_rows = mix_in.shape[0]
    grad_mix_in_shard = lax.dynamic_slice_in_dim(total_mix_in, dp_index * mixin_rows, mixin_rows, 0)
    mixout_cols = mix_out.shape[1]
    grad_mix_out_shard = lax.dynamic_slice_in_dim(
        total_mix_out, dp_index * mixout_cols, mixout_cols, 1
    )
    bias_cols = mix_bias.shape[0]
    grad_mix_bias_shard = lax.dynamic_slice_in_dim(
        total_mix_bias, dp_index * bias_cols, bias_cols, 0
    )
    return (
        new_streams,
        grad_streams,
        grad_prior,
        shard_qk,
        shard_value,
        shard_out,
        shard_up,
        shard_down,
        grad_norm_gain,
        grad_norm_bias,
        grad_mix_in_shard,
        grad_mix_out_shard,
        grad_mix_bias_shard,
    )


def solution(mesh):
    in_specs = (
        P(None, ("dp", "tensor"), None),
        P(None, ("dp", "tensor"), None),
        P("dp"),
        P("dp"),
        P(None, "dp", "tensor"),
        P("dp", "tensor"),
        P("tensor", "dp"),
        P("dp", "tensor"),
        P("tensor", "dp"),
        P(None, "dp"),
        P(None, "dp"),
        P("dp", None),
        P(None, "dp"),
        P("dp"),
        P(None, ("dp", "tensor"), None),
    )
    out_specs = (
        P(None, ("dp", "tensor"), None),
        P(None, ("dp", "tensor"), None),
        P(None, ("dp", "tensor"), None),
        P(None, "dp", "tensor"),
        P("dp", "tensor"),
        P("tensor", "dp"),
        P("dp", "tensor"),
        P("tensor", "dp"),
        P(None, "dp"),
        P(None, "dp"),
        P("dp", None),
        P(None, "dp"),
        P("dp"),
    )
    return jax.shard_map(body, mesh=mesh, in_specs=in_specs, out_specs=out_specs, check_vma=False)
```

profile of v0, /device:TPU:0, one launch (start us, length us, event | category | flops | bytes accessed | tf_op | source)
XLA Modules:
  0.0 2550.7 jit_solution(3912827108273020644)
XLA Ops:
  100.9 96.1 %all-gather.20.cloned.1.call-done = bf16[2560,2048]{1,0:T(8,128)(2,1)} async-done(((bf16[640,2048]{1,0:T(8,128)(2,1)}), bf16[2560,2048]{1,0:T(8,128)(2,1)}) %all-gather.20.cloned.1.call-update) | async-done | bytes 10485776 | tf_op jit(solution)/shard_map/all_gather | solution.py:123
  207.6 96.6 %all-gather.16.cloned.1.call-done = bf16[2560,2048]{1,0:T(8,128)(2,1)} async-done(((bf16[640,2048]{1,0:T(8,128)(2,1)}), bf16[2560,2048]{1,0:T(8,128)(2,1)}) %all-gather.16.cloned.1.call-update) | async-done | bytes 10485776 | tf_op jit(solution)/shard_map/all_gather | solution.py:122
  334.9 106.6 %all-gather.22.cloned.1.call-done = bf16[2560,2048]{1,0:T(8,128)(2,1)} async-done(((bf16[640,2048]{1,0:T(8,128)(2,1)}), bf16[2560,2048]{1,0:T(8,128)(2,1)}) %all-gather.22.cloned.1.call-update) | async-done | bytes 10485776 | tf_op jit(solution)/shard_map/all_gather | solution.py:124
  453.7 212.0 %while.27 = (s32[]{:T(128)}, bf16[5,512,4,128]{3,2,1,0:T(4,128)(2,1)}, f32[5,4,512,1]{2,1,3,0:T(4,128)}, s32[2560]{0:T(1024)S(1)}, s32[5]{0:T(128)}, /*index=5*/...) while((s32[]{:T(128)}, ...), condition=%wide.region_9.10_spmd, body=%wide.region_6.9_spmd.sunk | while | flops 2747531776 | bytes 164740368 | solution.py:173
  670.8 34.5 %all_to_all.70 = bf16[4,640,512]{2,1,0:T(8,128)(2,1)S(1)} all-to-all(bf16[4,640,512]{2,1,0:T(8,128)(2,1)} %all_to_all.52), channel_id=1, replica_groups=mesh['dp'=8,'tensor'=4] {'tensor'}, dimensions={0} | all-to-all | bytes 5242880 | tf_op jit(solution)/shard_map/all_to_all | solution.py:180
  723.3 103.8 %all-gather.30.cloned.1.call-done = bf16[2560,2048]{1,0:T(8,128)(2,1)} async-done(((bf16[640,2048]{1,0:T(8,128)(2,1)}), bf16[2560,2048]{1,0:T(8,128)(2,1)}) %all-gather.30.cloned.1.call-update) | async-done | bytes 10485776 | tf_op jit(solution)/shard_map/all_gather | solution.py:184
  827.1 71.1 %multiply_convert_fusion.1 = (bf16[2560,2048]{1,0:T(8,128)(2,1)}, f32[2560,2048]{1,0:T(8,128)}, f32[2560,2048]{1,0:T(8,128)}) fusion(bf16[2560,2048]{1,0:T(8,128)(2,1)} %all-gather.30.cloned.1.call-done, bf16[2048,2048]{1,0:T(8,128)(2,1)} %all-gather.32.cloned.1.call-done), kind=kOutput, calls=%fused_computation.49 | convolution fusion | flops 21815623680 | bytes 71303168 | tf_op jit(solution)/shard_map/dot_general | solution.py:185
  911.1 29.3 %fusion.98 = f32[2560,2048]{1,0:T(8,128)} fusion(bf16[2560,2048]{1,0:T(8,128)(2,1)} %get-tuple-element.425, bf16[2048,2048]{1,0:T(8,128)(2,1)} %all-gather.34.cloned.1.call-done), kind=kOutput, calls=%fused_computation.223 | convolution fusion | flops 21474836480 | bytes 39845888 | tf_op jit(solution)/shard_map/dot_general | solution.py:188
  990.8 135.7 %reduce-scatter.8.cloned.1.call-done = f32[640,2048]{1,0:T(8,128)} async-done(((f32[2560,2048]{1,0:T(8,128)}), f32[640,2048]{1,0:T(8,128)}) %reduce-scatter.8.cloned.1.call-update) | async-done | bytes 5242896 | tf_op jit(solution)/shard_map/reduce_scatter | solution.py:187
  1144.8 64.4 %fusion.97 = (f32[4,4]{0,1:T(4,128)}, f32[640,4,4]{1,2,0:T(4,128)S(1)}) fusion(bf16[4,640,2048]{2,1,0:T(8,128)(2,1)} %param.33, f32[4,640,2048]{2,1,0:T(8,128)} %pad_maximum_fusion), kind=kOutput, calls=%fused_computation.222 | convolution fusion | flops 251668464 | bytes 31498304 | tf_op jit(solution)/shard_map/srd,jrd->rsj/dot_general | solution.py:207
  1226.1 38.6 %fusion.49 = f32[640,4,2048]{2,1,0:T(4,128)} fusion(f32[640,4,4]{1,2,0:T(4,128)S(1)} %copy.148, bf16[4,640,2048]{2,1,0:T(8,128)(2,1)} %param.33), kind=kOutput, calls=%fused_computation.80 | convolution fusion | flops 251658240 | bytes 31498240 | tf_op jit(solution)/shard_map/rsj,srd->jrd/dot_general | solution.py:210
  1295.1 105.0 %all-gather.36.cloned.1.call-done = bf16[2560,2048]{1,0:T(8,128)(2,1)} async-done(((bf16[640,2048]{1,0:T(8,128)(2,1)}), bf16[2560,2048]{1,0:T(8,128)(2,1)}) %all-gather.36.cloned.1.call-update) | async-done | bytes 10485776 | tf_op jit(solution)/shard_map/all_gather | solution.py:233
  1400.1 38.2 %add_convert_fusion = bf16[2560,2048]{1,0:T(8,128)(2,1)} fusion(f32[2560,2048]{1,0:T(8,128)} %get-tuple-element.426, f32[2560,2048]{1,0:T(8,128)} %get-tuple-element.469, bf16[2560,2048]{1,0:T(8,128)(2,1)} %all-gather.36.cloned.1.call-done, bf16[2048,2048]{1,0:T(8,128)(2,1)} %all-gather.34.cloned.1.call-done), kind=kOutput, calls=%fused_computation.48 | convolution fusion | flops 21548236800 | bytes 71303168 | tf_op jit(solution)/shard_map/dot_general | solution.py:65
  1438.3 28.1 %convolution_convert_fusion = bf16[2560,2048]{1,0:T(8,128)(2,1)} fusion(bf16[2560,2048]{1,0:T(8,128)(2,1)} %add_convert_fusion, bf16[2048,2048]{1,0:T(8,128)(2,1)} %all-gather.32.cloned.1.call-done), kind=kOutput, calls=%fused_computation.68 | convolution fusion | flops 21480079360 | bytes 29360128 | tf_op jit(solution)/shard_map/dot_general | solution.py:65
  1466.7 103.3 %reduce-scatter.10.cloned.1.call-done = bf16[640,2048]{1,0:T(8,128)(2,1)} async-done(((bf16[2560,2048]{1,0:T(8,128)(2,1)}), bf16[640,2048]{1,0:T(8,128)(2,1)}) %reduce-scatter.10.cloned.1.call-update) | async-done | bytes 2621456 | tf_op jit(solution)/shard_map/reduce_scatter | solution.py:239
  1590.1 29.6 %convolution_convert_fusion.2 = bf16[2048,2048]{1,0:T(8,128)(2,1)} fusion(bf16[2560,2048]{1,0:T(8,128)(2,1)} %all-gather.30.cloned.1.call-done, bf16[2560,2048]{1,0:T(8,128)(2,1)} %add_convert_fusion), kind=kOutput, calls=%fused_computation.91 | convolution fusion | flops 21479030784 | bytes 29360128 | tf_op jit(solution)/shard_map/dot_general | solution.py:59
  1620.2 28.9 %convolution_convert_fusion.1 = bf16[2048,2048]{1,0:T(8,128)(2,1)} fusion(bf16[2560,2048]{1,0:T(8,128)(2,1)} %get-tuple-element.425, bf16[2560,2048]{1,0:T(8,128)(2,1)} %all-gather.36.cloned.1.call-done), kind=kOutput, calls=%fused_computation.90 | convolution fusion | flops 21479030784 | bytes 29360128 | tf_op jit(solution)/shard_map/dot_general | solution.py:59
  1649.2 43.2 %all-gather.38.cloned.1.call-done = bf16[2560,2048]{1,0:T(8,128)(2,1)} async-done(((bf16[640,2048]{1,0:T(8,128)(2,1)}), bf16[2560,2048]{1,0:T(8,128)(2,1)}) %all-gather.38.cloned.1.call-update) | async-done | bytes 10485776 | tf_op jit(solution)/shard_map/all_gather | solution.py:249
  1703.2 419.1 %while.28 = (s32[]{:T(128)}, f32[2560,4,128]{0,2,1:T(8,128)}, f32[2560,4,128]{0,2,1:T(8,128)}, f32[5,512,4,128]{3,1,0,2:T(8,128)}, s32[5]{0:T(128)S(1)}, /*index...) while((s32[]{:T(128)}, f32[2560,4,128]{0,2,1:T(8,128)}, ...), condition=%wide.region_22.23_spmd.clone, body=%wide.region_20.22_spmd.clone.sunk | while | flops 6801588736 | bytes 226073968 | solution.py:288
  1988.4 20.2 multiply_convert_fusion.3
  2072.0 20.3 multiply_convert_fusion.3
  2341.0 57.1 %convert_bitcast_fusion = bf16[4,640,2048]{2,0,1:T(4,128)(2,1)} fusion(f32[640,4,4]{1,2,0:T(4,128)S(1)} %copy-done.12, f32[4,640,2048]{2,1,0:T(8,128)} %pad_maximum_fusion), kind=kOutput, calls=%fused_computation.74 | convolution fusion | flops 256901120 | bytes 31498240 | tf_op jit(solution)/shard_map/rsj,jrd->srd/dot_general | solution.py:204
  2455.5 35.2 %reduce-scatter.16.cloned.1.call-done = bf16[512,256]{1,0:T(8,128)(2,1)} async-done(((bf16[512,2048]{1,0:T(8,128)(2,1)}), bf16[512,256]{1,0:T(8,128)(2,1)}) %reduce-scatter.16.cloned.1.call-update) | async-done | bytes 262160 | tf_op jit(solution)/shard_map/reduce_scatter | solution.py:328
  2492.5 49.1 %reduce-scatter.12.cloned.1.call-done = bf16[2,256,512]{2,1,0:T(8,128)(2,1)} async-done(((bf16[2,2048,512]{2,1,0:T(8,128)(2,1)}), bf16[2,256,512]{2,1,0:T(8,128)(2,1)}) %reduce-scatter.12.cloned.1.call-update) | async-done | bytes 524304 | tf_op jit(solution)/shard_map/reduce_scatter | solution.py:322
  (510 shorter events, 1182.2 us)
Async XLA Ops:
  7.2 71.5 %all-gather.26.cloned.1.call-start = ((), (), s32[]{:S(2)}) async-start(), calls=%async_computation.16 | async-start | bytes 2359296 | tf_op jit(solution)/shard_map/all_gather | solution.py:106
  7.9 82.9 %all-gather.18.cloned.1.call-start = ((), (), s32[]{:S(2)}) async-start(), calls=%async_computation.12 | async-start | bytes 4718592 | tf_op jit(solution)/shard_map/all_gather | solution.py:104
  8.7 188.3 %all-gather.20.cloned.1.call-start = ((), (), s32[]{:S(2)}) async-start(), calls=%async_computation.13 | async-start | bytes 13107200 | tf_op jit(solution)/shard_map/all_gather | solution.py:123
  76.9 227.3 %all-gather.16.cloned.1.call-start = ((), (), s32[]{:S(2)}) async-start(), calls=%async_computation.11 | async-start | bytes 13107200 | tf_op jit(solution)/shard_map/all_gather | solution.py:122
  77.5 257.4 %all-gather.24.cloned.1.call-start = ((), (), s32[]{:S(2)}) async-start(), calls=%async_computation.15 | async-start | bytes 2359296 | tf_op jit(solution)/shard_map/all_gather | solution.py:105
  78.1 363.4 %all-gather.22.cloned.1.call-start = ((), (), s32[]{:S(2)}) async-start(), calls=%async_computation.14 | async-start | bytes 13107200 | tf_op jit(solution)/shard_map/all_gather | solution.py:124
  78.7 629.2 %all-gather.28.cloned.1.call-start = ((), (), s32[]{:S(2)}) async-start(), calls=%async_computation.17 | async-start | bytes 10485760 | tf_op jit(solution)/shard_map/all_gather | solution.py:178
  79.4 643.9 %all-gather.32.cloned.1.call-start = ((), (), s32[]{:S(2)}) async-start(), calls=%async_computation.19 | async-start | bytes 9437184 | tf_op jit(solution)/shard_map/all_gather | solution.py:107
  80.2 747.0 %all-gather.30.cloned.1.call-start = ((), (), s32[]{:S(2)}) async-start(), calls=%async_computation.18 | async-start | bytes 13107200 | tf_op jit(solution)/shard_map/all_gather | solution.py:184
  722.7 188.4 %all-gather.34.cloned.1.call-start = ((), (), s32[]{:S(2)}) async-start(), calls=%async_computation.20 | async-start | bytes 9437184 | tf_op jit(solution)/shard_map/all_gather | solution.py:108
  723.3 403.2 %reduce-scatter.8.cloned.1.call-start = ((), (), s32[]{:S(2)}) async-start(), calls=%async_computation.21 | async-start | bytes 26214400 | tf_op jit(solution)/shard_map/reduce_scatter | solution.py:187
  940.4 459.7 %all-gather.36.cloned.1.call-start = ((), (), s32[]{:S(2)}) async-start(), calls=%async_computation.22 | async-start | bytes 13107200 | tf_op jit(solution)/shard_map/all_gather | solution.py:233
  1295.0 275.0 %reduce-scatter.10.cloned.1.call-start = ((), (), s32[]{:S(2)}) async-start(), calls=%async_computation.23 | async-start | bytes 13107200 | tf_op jit(solution)/shard_map/reduce_scatter | solution.py:239
  1466.4 225.9 %all-gather.38.cloned.1.call-start = ((), (), s32[]{:S(2)}) async-start(), calls=%async_computation.24 | async-start | bytes 13107200 | tf_op jit(solution)/shard_map/all_gather | solution.py:249
  1587.2 646.5 %all-gather.40.cloned.1.call-start = ((), (), s32[]{:S(2)}) async-start(), calls=%async_computation.25 | async-start | bytes 20971520 | tf_op jit(solution)/shard_map/all_gather | solution.py:176
  1587.8 680.6 %all-gather.42.cloned.1.call-start = ((), (), s32[]{:S(2)}) async-start(), calls=%async_computation.26 | async-start | bytes 10485760 | tf_op jit(solution)/shard_map/all_gather | solution.py:177
  1588.4 823.6 %all-reduce.5.cloned.1.call-start = ((), (), s32[]{:S(2)}) async-start(), calls=%async_computation.32 | async-start | bytes 262144 | tf_op jit(solution)/shard_map/psum | solution.py:340
  1590.1 823.2 %reduce-scatter.18.cloned.1.call-start = ((), (), s32[]{:S(2)}) async-start(), calls=%async_computation.30 | async-start | bytes 9437184 | tf_op jit(solution)/shard_map/reduce_scatter | solution.py:331
  1619.8 796.3 %reduce-scatter.20.cloned.1.call-start = ((), (), s32[]{:S(2)}) async-start(), calls=%async_computation.31 | async-start | bytes 9437184 | tf_op jit(solution)/shard_map/reduce_scatter | solution.py:334
  2153.0 35.5 %all-to-all-start.2 = ((bf16[4,640,512]{1,2,0:T(8,128)(2,1)}), bf16[4,640,512]{1,2,0:T(8,128)(2,1)}, u32[]{:S(2)}, u32[]{:S(2)}) async-start(bf16[4,640,512]{1,2,0:T(8,128)(2,1)} %copy.162), calls=%async_computation.4 | async-start | bytes 5242880 | tf_op jit(solution)/shard_map/all_to_all | solution.py:309
  2227.8 210.0 %all-reduce.7.cloned.1.call-start = ((), (), s32[]{:S(2)}) async-start(), calls=%async_computation.33 | async-start | bytes 279552 | tf_op jit(solution)/shard_map/psum | solution.py:340
  2289.2 164.5 %reduce-scatter.14.cloned.1.call-start = ((), (), s32[]{:S(2)}) async-start(), calls=%async_computation.28 | async-start | bytes 2359296 | tf_op jit(solution)/shard_map/reduce_scatter | solution.py:325
  2301.2 189.5 %reduce-scatter.16.cloned.1.call-start = ((), (), s32[]{:S(2)}) async-start(), calls=%async_computation.29 | async-start | bytes 2359296 | tf_op jit(solution)/shard_map/reduce_scatter | solution.py:328
  2311.4 230.2 %reduce-scatter.12.cloned.1.call-start = ((), (), s32[]{:S(2)}) async-start(), calls=%async_computation.27 | async-start | bytes 4718592 | tf_op jit(solution)/shard_map/reduce_scatter | solution.py:322
  (104 other events, 2104.7 us)
Sparse Core Ops, SparseCore 0:
  9.6 33.5 all-gather.25
  44.8 46.0 all-gather.17
  93.2 103.7 all-gather.19
  199.3 104.9 all-gather.15
  305.7 29.1 all-gather.23
  337.1 104.3 all-gather.21
  443.3 87.4 all-gather.27
  532.4 82.0 all-gather.31
  722.8 104.3 all-gather.29
  828.6 82.4 all-gather.33
  940.5 185.9 reduce-scatter.7
  1295.1 104.9 all-gather.35
  1466.5 103.4 reduce-scatter.9
  1587.4 104.8 all-gather.37
  1694.0 157.1 all-gather.39
  1852.8 87.3 all-gather.41
  1946.2 124.3 all-reduce.4
  2072.8 88.5 reduce-scatter.17
  2163.7 87.9 reduce-scatter.19
  2289.3 122.9 all-reduce.6
  2414.6 39.0 reduce-scatter.13
  2456.0 34.6 reduce-scatter.15
  2493.0 48.5 reduce-scatter.11
where the time goes:
time: 2560 us; the launch traced here: 2550 us
  waiting for transfers between devices  970 us (38%)
  matrix products  921 us (36%)
  other arithmetic  322 us (13%)
  local copies, waits for them, and re-layouts  186 us (7%)
  blocking collectives  102 us (4%)
    reduce_scatter x1, waiting for transfers between devices, body(): lax.psum_scatter(jnp.dot(hidden, down_all, preferred_element_type=jnp.flo...  136 us
    dot_general x10, matrix products, block_scores(): jnp.einsum('qhe,khe->hqk', query_block, key_rot, preferred_element_type=j...  128 us
    dot_general x7, matrix products, contract_last(): lax.dot_general(left, right, (((1,), (1,)), ((), ())), preferred_element_...  123 us
    all_gather x1, waiting for transfers between devices, body(): lax.all_gather(normed_v, 'tensor', axis=0, tiled=True)  107 us
    all_gather x1, waiting for transfers between devices, body(): lax.all_gather(grad_layer.astype(jnp.bfloat16), 'tensor', axis=0, tiled=T...  105 us
    all_gather x1, waiting for transfers between devices, body(): mlp_rows = lax.all_gather(mlp_input, 'tensor', axis=0, tiled=True)  104 us
    reduce_scatter x1, waiting for transfers between devices, body(): lax.psum_scatter(contract_last(grad_hidden_pre, up_all).astype(jnp.bfloat...  103 us
    convert_element_type x5, other arithmetic, backward_block(): grad_scores = (block_probs * (grad_probs - row_inner)).astype(jnp.bfloat16)  101 us
  transfers between devices with their start and end apart: 26, of which 17 were waited for; matrix products, arithmetic and copies ran while one was open for 44% of the time, Pallas kernels for 0%

commit v1 on v0

v1 whole, which is shorter than its diff:
```python
import functools
import math

import jax
import jax.numpy as jnp
from jax import lax
from jax.experimental import pallas as pl
from jax.experimental.pallas import tpu as pltpu
from jax.sharding import PartitionSpec as P

HDIM = 128
MASKED_SCORE = -1e30
SCORE_SCALE = 1.0 / math.sqrt(HDIM)
LOG2_SCALE = SCORE_SCALE * math.log2(math.e)

def dot_nt(a, b):
    return lax.dot_general(a, b, (((1,), (1,)), ((), ())), preferred_element_type=jnp.float32)

def dot_nn(a, b):
    return lax.dot_general(a, b, (((1,), (0,)), ((), ())), preferred_element_type=jnp.float32)

def seen(pos_col, seg_col, pos_row, seg_row):
    return ((seg_col == 0) | (seg_col == seg_row)) & (pos_col <= pos_row)

def attend_kernel(block, q_ref, k_ref, v_ref, pc_ref, sc_ref, pr_ref, sr_ref, o_ref, l_ref, vt_ref):
    index = pl.program_id(1)

    @pl.when(index == 0)
    def _():
        vt_ref[...] = v_ref[...].T

    query = q_ref[...]

    def step(first, state, masked):
        top, total, acc = state
        rows = pl.ds(pl.multiple_of(first, block), block)
        scores = dot_nt(k_ref[rows, :], query) * LOG2_SCALE
        if masked:
            pairs = seen(pc_ref[rows, :], sc_ref[rows, :], pr_ref[...], sr_ref[...])
            scores = jnp.where(pairs, scores, MASKED_SCORE)
        new_top = jnp.maximum(top, jnp.max(scores, axis=0, keepdims=True))
        fade = jnp.exp2(top - new_top)
        probs = jnp.exp2(scores - new_top)
        total = total * fade + jnp.sum(probs, axis=0, keepdims=True)
        acc = acc * fade + dot_nn(vt_ref[:, rows], probs.astype(jnp.bfloat16))
        return new_top, total, acc

    state = (
        jnp.full((1, block), MASKED_SCORE, jnp.float32),
        jnp.zeros((1, block), jnp.float32),
        jnp.zeros((HDIM, block), jnp.float32),
    )
    state = lax.fori_loop(0, index, lambda j, s: step(j * block, s, False), state)
    top, total, acc = step(index * block, state, True)
    o_ref[...] = (acc / total).T.astype(jnp.bfloat16)
    l_ref[0] = top + jnp.log2(total)

def attend(q, k, v, pos, seg, block=512):
    rows, cols = q.shape
    heads = cols // HDIM
    grid = (heads, rows // block)
    tile = pl.BlockSpec((block, HDIM), lambda h, i: (i, h))
    whole = pl.BlockSpec((rows, HDIM), lambda h, i: (0, h))
    col = pl.BlockSpec((rows, 1), lambda h, i: (0, 0))
    row = pl.BlockSpec((1, block), lambda h, i: (0, i))
    return pl.pallas_call(
        functools.partial(attend_kernel, block),
        grid=grid,
        in_specs=[tile, whole, whole, col, col, row, row],
        out_specs=[tile, pl.BlockSpec((1, 1, block), lambda h, i: (h, 0, i))],
        out_shape=[
            jax.ShapeDtypeStruct((rows, cols), jnp.bfloat16),
            jax.ShapeDtypeStruct((heads, 1, rows), jnp.float32),
        ],
        scratch_shapes=[pltpu.VMEM((HDIM, rows), jnp.bfloat16)],
        cost_estimate=pl.CostEstimate(flops=30_000_000_000, bytes_accessed=4 * rows * cols * 2, transcendentals=0),
        name="attend",
    )(q, k, v, pos[:, None], seg[:, None], pos[None, :], seg[None, :])

def attend_back_kernel(block, q_ref, k_ref, v_ref, o_ref, go_ref, l_ref, pc_ref, sc_ref, pr_ref, sr_ref,
                       ck_ref, sk_ref, cq_ref, sq_ref, dq_ref, dk_ref, dv_ref, kt_ref, ak_ref, av_ref):
    index = pl.program_id(1)

    @pl.when(index == 0)
    def _():
        kt_ref[...] = k_ref[...].T

    query = q_ref[...]
    grad = go_ref[...]
    delta = jnp.sum((o_ref[...].astype(jnp.float32) * grad.astype(jnp.float32)).T, axis=0, keepdims=True)
    logs = l_ref[0]

    def step(first, acc, masked):
        rows = pl.ds(pl.multiple_of(first, block), block)
        scores = dot_nt(k_ref[rows, :], query) * LOG2_SCALE
        if masked:
            pairs = seen(pc_ref[rows, :], sc_ref[rows, :], pr_ref[...], sr_ref[...])
            scores = jnp.where(pairs, scores, MASKED_SCORE)
        probs = jnp.exp2(scores - logs)
        slopes = dot_nt(v_ref[rows, :], grad)
        turned = (probs * (slopes - delta)).astype(jnp.bfloat16)
        add_k = dot_nn(turned, query)
        add_v = dot_nn(probs.astype(jnp.bfloat16), grad)
        if masked:
            ak_ref[rows, :] = add_k
            av_ref[rows, :] = add_v
        else:
            ak_ref[rows, :] += add_k
            av_ref[rows, :] += add_v
        return acc + dot_nn(kt_ref[:, rows], turned)

    acc = lax.fori_loop(0, index, lambda j, s: step(j * block, s, False), jnp.zeros((HDIM, block), jnp.float32))
    acc = step(index * block, acc, True)

    def unturn(value, cosine, sine):
        value = value * SCORE_SCALE
        return (value * cosine - pltpu.roll(value, HDIM // 2, 1) * sine).astype(jnp.bfloat16)

    dq_ref[...] = unturn(acc.T, cq_ref[...], sq_ref[...])

    @pl.when(index == pl.num_programs(1) - 1)
    def _():
        @pl.loop(0, pl.num_programs(1))
        def _(j):
            rows = pl.ds(pl.multiple_of(j * block, block), block)
            dk_ref[rows, :] = unturn(ak_ref[rows, :], ck_ref[rows, :], sk_ref[rows, :])
            dv_ref[rows, :] = av_ref[rows, :].astype(jnp.bfloat16)

def attend_back(q, k, v, o, go, logs, pos, seg, cos2, sin2, block=512):
    rows, cols = q.shape
    heads = cols // HDIM
    grid = (heads, rows // block)
    tile = pl.BlockSpec((block, HDIM), lambda h, i: (i, h))
    whole = pl.BlockSpec((rows, HDIM), lambda h, i: (0, h))
    col = pl.BlockSpec((rows, 1), lambda h, i: (0, 0))
    row = pl.BlockSpec((1, block), lambda h, i: (0, i))
    table = pl.BlockSpec((rows, HDIM), lambda h, i: (0, 0))
    table_tile = pl.BlockSpec((block, HDIM), lambda h, i: (i, 0))
    like = jax.ShapeDtypeStruct((rows, cols), jnp.bfloat16)
    return pl.pallas_call(
        functools.partial(attend_back_kernel, block),
        grid=grid,
        in_specs=[tile, whole, whole, tile, tile, pl.BlockSpec((1, 1, block), lambda h, i: (h, 0, i)),
                  col, col, row, row, table, table, table_tile, table_tile],
        out_specs=[tile, whole, whole],
        out_shape=[like, like, like],
        scratch_shapes=[pltpu.VMEM((HDIM, rows), jnp.bfloat16), pltpu.VMEM((rows, HDIM), jnp.float32),
                        pltpu.VMEM((rows, HDIM), jnp.float32)],
        cost_estimate=pl.CostEstimate(flops=80_000_000_000, bytes_accessed=8 * rows * cols * 2, transcendentals=0),
        name="attend_back",
    )(q, k, v, o, go, logs, pos[:, None], seg[:, None], pos[None, :], seg[None, :], cos2, sin2, cos2, sin2)

EPSILON = 1e-05
HIGHEST_PRECISION = lax.Precision.HIGHEST
ROOT_HALF = math.sqrt(0.5)
PDF_SCALE = 1.0 / math.sqrt(2.0 * math.pi)

def gelu_pair(u):
    cdf = 0.5 + 0.5 * lax.erf(u * ROOT_HALF)
    return u * cdf, cdf + u * (PDF_SCALE * jnp.exp(-0.5 * u * u))

def exact_dot(a, b, dims):
    return lax.dot_general(a, b, (dims, ((), ())), precision=HIGHEST_PRECISION, preferred_element_type=jnp.float32)

def low_dot(a, b, dims):
    return lax.dot_general(a, b, (dims, ((), ())), preferred_element_type=jnp.float32)

def standard(x):
    width = x.shape[-1]
    centre = x - jnp.sum(x, axis=-1, keepdims=True) * (1.0 / width)
    spread = jnp.sum(centre * centre, axis=-1, keepdims=True) * (1.0 / width)
    rstd = lax.rsqrt(spread + EPSILON)
    return centre * rstd, rstd

def pull_standard(xhat, rstd, w):
    width = xhat.shape[-1]
    mean_w = jnp.sum(w, axis=-1, keepdims=True) * (1.0 / width)
    mean_wx = jnp.sum(w * xhat, axis=-1, keepdims=True) * (1.0 / width)
    return (w - mean_w - xhat * mean_wx) * rstd

def row_tile(rows, most):
    tile = min(most, rows)
    while rows % tile:
        tile -= 16
    return tile

def norm_kernel(x_ref, gain_ref, shift_ref, n_ref):
    xhat, _ = standard(x_ref[0].astype(jnp.float32))
    n_ref[0] = (xhat * gain_ref[0] + shift_ref[0]).astype(jnp.bfloat16)

def norm_streams(x, count, gains, shifts):
    rows, width = x.shape[1:]
    tile = row_tile(rows, 128)
    block = pl.BlockSpec((1, tile, width), lambda s, i: (s, i, 0))
    vec = pl.BlockSpec((1, 1, width), lambda s, i: (s, 0, 0))
    return pl.pallas_call(
        norm_kernel, grid=(count, rows // tile), in_specs=[block, vec, vec], out_specs=block,
        out_shape=jax.ShapeDtypeStruct((count, rows, width), jnp.bfloat16), name="norm_streams",
    )(x, gains[:, None, :], shifts[:, None, :])

def mixer_kernel(mid_ref, part_ref, left_ref, right_ref, prior_ref, up_ref, gain_ref, shift_ref,
                 mixin_ref, mixout_ref, bias_ref,
                 new_ref, gprior_ref, gout_ref, gz_ref, gin_ref, gmo_ref, gmb_ref, gg_ref, gs_ref):
    first = pl.program_id(0) == 0
    sources = prior_ref.shape[0] + 1
    count = up_ref.shape[0]
    tile = mid_ref.shape[0]
    wide = count * sources
    out = mid_ref[...] + part_ref[...].astype(jnp.float32) + left_ref[...].astype(jnp.float32) + right_ref[...].astype(jnp.float32)
    xhat, rstd = standard(out)
    gain = gain_ref[...]
    c = (xhat * gain + shift_ref[...]).astype(jnp.bfloat16)
    g = low_dot(c, mixin_ref[...], ((1,), (1,)))
    act, slope = gelu_pair(g)
    coef = exact_dot(act, mixout_ref[...], ((1,), (0,))) + bias_ref[...]
    x = [prior_ref[j].astype(jnp.float32) for j in range(sources - 1)] + [out]
    u = [up_ref[s].astype(jnp.float32) for s in range(count)]
    co = [[coef[:, s * sources + j : s * sources + j + 1] for j in range(sources)] for s in range(count)]
    lane = lax.broadcasted_iota(jnp.int32, (tile, wide), 1)
    gcoef = jnp.zeros((tile, wide), jnp.float32)
    for s in range(count):
        mixed = co[s][0] * x[0]
        for j in range(1, sources):
            mixed = mixed + co[s][j] * x[j]
        new_ref[s] = mixed.astype(jnp.bfloat16)
        for j in range(sources):
            inner = jnp.sum(u[s] * x[j], axis=-1, keepdims=True)
            gcoef = jnp.where(lane == s * sources + j, inner, gcoef)
    for j in range(sources):
        total = co[0][j] * u[0]
        for s in range(1, count):
            total = total + co[s][j] * u[s]
        if j < sources - 1:
            gprior_ref[j] = total.astype(jnp.bfloat16)
    gact = exact_dot(gcoef, mixout_ref[...], ((1,), (1,)))
    gg = (gact * slope).astype(jnp.bfloat16)
    gc = low_dot(gg, mixin_ref[...], ((1,), (0,)))
    gout = total + pull_standard(xhat, rstd, gc * gain)
    gout_ref[...] = gout
    gz_ref[...] = gout.astype(jnp.bfloat16)

    @pl.when(first)
    def _():
        for ref in (gin_ref, gmo_ref, gmb_ref, gg_ref, gs_ref):
            ref[...] = jnp.zeros_like(ref)

    gin_ref[...] += low_dot(gg, c, ((0,), (0,)))
    gmo_ref[...] += exact_dot(act, gcoef, ((0,), (0,)))
    gmb_ref[...] += jnp.sum(gcoef, axis=0, keepdims=True)
    gg_ref[...] += jnp.sum(gc * xhat, axis=0, keepdims=True)
    gs_ref[...] += jnp.sum(gc, axis=0, keepdims=True)

def mixer(mid, parts, prior, d_streams, gain, shift, mix_in, mix_out, mix_bias, most=64):
    rows, width = mid.shape
    hidden = mix_in.shape[0]
    wide = mix_out.shape[1]
    tile = row_tile(rows, most)
    flat = pl.BlockSpec((tile, width), lambda i: (i, 0))
    stack = lambda n: pl.BlockSpec((n, tile, width), lambda i: (0, i, 0))
    full = lambda *s: pl.BlockSpec(s, lambda i: (0,) * len(s))
    f32 = jnp.float32
    shape = jax.ShapeDtypeStruct
    return pl.pallas_call(
        mixer_kernel, grid=(rows // tile,),
        in_specs=[flat, flat, flat, flat, stack(prior.shape[0]), stack(d_streams.shape[0]),
                  full(1, width), full(1, width), full(hidden, width), full(hidden, wide), full(1, wide)],
        out_specs=[stack(d_streams.shape[0]), stack(prior.shape[0]), flat, flat,
                   full(hidden, width), full(hidden, wide), full(1, wide), full(1, width), full(1, width)],
        out_shape=[shape(d_streams.shape, jnp.bfloat16), shape(prior.shape, jnp.bfloat16),
                   shape((rows, width), f32), shape((rows, width), jnp.bfloat16),
                   shape((hidden, width), f32), shape((hidden, wide), f32), shape((1, wide), f32),
                   shape((1, width), f32), shape((1, width), f32)],
        cost_estimate=pl.CostEstimate(flops=1000000, bytes_accessed=60_000_000, transcendentals=0),
        name="mixer",
    )(mid, *parts, prior, d_streams, gain[None], shift[None], mix_in, mix_out, mix_bias[None])

def middle_kernel(attn_ref, stream_ref, gain_ref, shift_ref, mid_ref, m_ref):
    mid = attn_ref[...] + stream_ref[0].astype(jnp.float32)
    mid_ref[...] = mid
    xhat, _ = standard(mid)
    m_ref[...] = (xhat * gain_ref[...] + shift_ref[...]).astype(jnp.bfloat16)

def middle(attn, streams, gain, shift):
    rows, width = attn.shape
    tile = row_tile(rows, 128)
    flat = pl.BlockSpec((tile, width), lambda i: (i, 0))
    vec = pl.BlockSpec((1, width), lambda i: (0, 0))
    return pl.pallas_call(
        middle_kernel, grid=(rows // tile,),
        in_specs=[flat, pl.BlockSpec((1, tile, width), lambda i: (3, i, 0)), vec, vec],
        out_specs=[flat, flat],
        out_shape=[jax.ShapeDtypeStruct((rows, width), jnp.float32), jax.ShapeDtypeStruct((rows, width), jnp.bfloat16)],
        name="middle",
    )(attn, streams, gain[None], shift[None])

def middle_back(mid, gout, parts, gain):
    rows, width = mid.shape
    tile = row_tile(rows, 64)
    flat = pl.BlockSpec((tile, width), lambda i: (i, 0))
    vec = pl.BlockSpec((1, width), lambda i: (0, 0))
    shape = jax.ShapeDtypeStruct
    return pl.pallas_call(
        middle_back_kernel, grid=(rows // tile,),
        in_specs=[flat] * 5 + [vec], out_specs=[flat, vec, vec],
        out_shape=[shape((rows, width), jnp.bfloat16), shape((1, width), jnp.float32), shape((1, width), jnp.float32)],
        name="middle_back",
    )(mid, gout, *parts, gain[None])

def middle_back_kernel(mid_ref, gout_ref, part_ref, left_ref, right_ref, gain_ref, low_ref, gg_ref, gs_ref):
    xhat, rstd = standard(mid_ref[...])
    r = part_ref[...].astype(jnp.float32) + left_ref[...].astype(jnp.float32) + right_ref[...].astype(jnp.float32)
    low_ref[...] = (gout_ref[...] + pull_standard(xhat, rstd, r * gain_ref[...])).astype(jnp.bfloat16)

    @pl.when(pl.program_id(0) == 0)
    def _():
        gg_ref[...] = jnp.zeros_like(gg_ref)
        gs_ref[...] = jnp.zeros_like(gs_ref)

    gg_ref[...] += jnp.sum(r * xhat, axis=0, keepdims=True)
    gs_ref[...] += jnp.sum(r, axis=0, keepdims=True)

def streams_back_kernel(x_ref, rq_ref, rk_ref, rv_ref, last_ref, gain_ref, gx_ref, gg_ref, gs_ref):
    @pl.when(pl.program_id(0) == 0)
    def _():
        gg_ref[...] = jnp.zeros_like(gg_ref)
        gs_ref[...] = jnp.zeros_like(gs_ref)

    for s, ref in enumerate((rq_ref, rk_ref, rv_ref)):
        xhat, rstd = standard(x_ref[s].astype(jnp.float32))
        r = ref[...]
        gx_ref[s] = pull_standard(xhat, rstd, r * gain_ref[s]).astype(jnp.bfloat16)
        gg_ref[s] += jnp.sum(r * xhat, axis=0, keepdims=True)
        gs_ref[s] += jnp.sum(r, axis=0, keepdims=True)
    gx_ref[3] = last_ref[...]

def streams_back(x, rq, rk, rv, last, gains):
    rows, width = rq.shape
    tile = row_tile(rows, 64)
    flat = pl.BlockSpec((tile, width), lambda i: (i, 0))
    three = pl.BlockSpec((3, 1, width), lambda i: (0, 0, 0))
    shape = jax.ShapeDtypeStruct
    return pl.pallas_call(
        streams_back_kernel, grid=(rows // tile,),
        in_specs=[pl.BlockSpec((3, tile, width), lambda i: (0, i, 0)), flat, flat, flat, flat, three],
        out_specs=[pl.BlockSpec((4, tile, width), lambda i: (0, i, 0)), three, three],
        out_shape=[shape((4, rows, width), jnp.bfloat16), shape((3, 1, width), jnp.float32), shape((3, 1, width), jnp.float32)],
        name="streams_back",
    )(x, rq, rk, rv, last, gains[:, None, :])

def project_kernel(turn, swap, n_ref, w_ref, *rest):
    if turn:
        c_ref, s_ref, o_ref = rest
    else:
        (o_ref,) = rest
    y = low_dot(n_ref[...], w_ref[0], ((1,), (1 if swap else 0,)))
    if turn:
        for h in range(y.shape[1] // 128):
            cols = slice(h * 128, (h + 1) * 128)
            part = y[:, cols]
            o_ref[0, :, cols] = (part * c_ref[...] + pltpu.roll(part, 64, 1) * s_ref[...]).astype(jnp.bfloat16)
    else:
        o_ref[0] = y.astype(jnp.bfloat16)

def project(n, w4, tables=None, swap=False, name="project"):
    rows, width = n.shape
    groups = w4.shape[0]
    cols = w4.shape[1] if swap else w4.shape[2]
    specs = [pl.BlockSpec((rows, width), lambda g: (0, 0)), pl.BlockSpec((1,) + w4.shape[1:], lambda g: (g, 0, 0))]
    args = [n, w4]
    if tables is not None:
        specs += [pl.BlockSpec((rows, 128), lambda g: (0, 0))] * 2
        args += list(tables)
    return pl.pallas_call(
        functools.partial(project_kernel, tables is not None, swap), grid=(groups,),
        in_specs=specs, out_specs=pl.BlockSpec((1, rows, cols), lambda g: (g, 0, 0)),
        out_shape=jax.ShapeDtypeStruct((groups, rows, cols), jnp.bfloat16),
        cost_estimate=pl.CostEstimate(flops=2 * rows * width * cols * groups, bytes_accessed=w4.size * 2, transcendentals=0),
        name=name,
    )(*args)

def join_kernel(swap, a_ref, w_ref, o_ref):
    total = None
    for g in range(a_ref.shape[0]):
        part = low_dot(a_ref[g], w_ref[g], ((1,), (1 if swap else 0,)))
        total = part if total is None else total + part
    o_ref[...] = total

def join(a4, w4, swap=False, name="join"):
    groups, rows, cols = a4.shape
    width = w4.shape[1] if swap else w4.shape[2]
    tile = 512
    if swap:
        spec = pl.BlockSpec((groups, tile, cols), lambda i: (0, i, 0))
    else:
        spec = pl.BlockSpec((groups, cols, tile), lambda i: (0, 0, i))
    return pl.pallas_call(
        functools.partial(join_kernel, swap), grid=(width // tile,),
        in_specs=[pl.BlockSpec((groups, rows, cols), lambda i: (0, 0, 0)), spec],
        out_specs=pl.BlockSpec((rows, tile), lambda i: (0, i)),
        out_shape=jax.ShapeDtypeStruct((rows, width), jnp.float32),
        cost_estimate=pl.CostEstimate(flops=2 * rows * width * cols * groups, bytes_accessed=w4.size * 2, transcendentals=0),
        name=name,
    )(a4, w4)

def weight_kernel(swap, n_ref, a_ref, o_ref, t_ref):
    if swap:
        o_ref[0] = low_dot(a_ref[0].T, n_ref[...], ((1,), (0,))).astype(jnp.bfloat16)
    else:
        @pl.when(pl.program_id(0) == 0)
        def _():
            t_ref[...] = n_ref[...].T
        o_ref[0] = low_dot(t_ref[...], a_ref[0], ((1,), (0,))).astype(jnp.bfloat16)

def weight_grad(n, a4, swap=False, name="weight_grad"):
    rows, width = n.shape
    groups, _, cols = a4.shape
    out = (cols, width) if swap else (width, cols)
    return pl.pallas_call(
        functools.partial(weight_kernel, swap), grid=(groups,),
        in_specs=[pl.BlockSpec((rows, width), lambda g: (0, 0)), pl.BlockSpec((1, rows, cols), lambda g: (g, 0, 0))],
        out_specs=pl.BlockSpec((1,) + out, lambda g: (g, 0, 0)),
        out_shape=jax.ShapeDtypeStruct((groups,) + out, jnp.bfloat16),
        scratch_shapes=[pltpu.VMEM((8, 128) if swap else (width, rows), jnp.bfloat16)],
        cost_estimate=pl.CostEstimate(flops=2 * rows * width * cols * groups, bytes_accessed=groups * width * cols * 2, transcendentals=0),
        name=name,
    )(n, a4)


def rotary_tables(position_row):
    half_width = HDIM // 2
    frequency = jnp.exp(
        jnp.arange(half_width, dtype=jnp.float32) * (-2.0 * math.log(10000.0) / HDIM)
    )
    angles = position_row.astype(jnp.float32)[:, None] * frequency[None, :]
    cosine, sine = jnp.cos(angles), jnp.sin(angles)
    return jnp.concatenate([cosine, cosine], axis=1), jnp.concatenate([-sine, sine], axis=1)


def hop(value, mask):
    size = lax.axis_size("tensor")
    return lax.ppermute(value, "tensor", [(i, i ^ mask) for i in range(size)])


def spread_rows(own):
    if lax.axis_size("tensor") != 4:
        return [lax.all_gather(own, "tensor", axis=0, tiled=True)]
    half = own.shape[0] // 2
    one, two = hop(own, 1), hop(own, 2)
    return [own, one, two, hop(one[:half], 2), hop(two[half:], 1)]


def collect_rows(pieces):
    if lax.axis_size("tensor") != 4:
        total = lax.psum_scatter(pieces[0], "tensor", scatter_dimension=0, tiled=True)
        zero = jnp.zeros_like(total)
        return total, zero, zero
    own, one, two, far_low, far_high = pieces
    half = own.shape[0] // 2
    low = hop(far_low, 1)
    high = hop(far_high, 2)
    f32 = jnp.float32
    two = jnp.concatenate(
        [(two[:half].astype(f32) + low.astype(f32)).astype(jnp.bfloat16), two[half:]]
    )
    one = jnp.concatenate(
        [one[:half], (one[half:].astype(f32) + high.astype(f32)).astype(jnp.bfloat16)]
    )
    return own, hop(one, 1), hop(two, 2)


def sum_tensor(value):
    if lax.axis_size("tensor") != 4:
        return lax.psum(value, "tensor")
    value = value + hop(value, 1)
    return value + hop(value, 2)


def exchange(value):
    return lax.all_to_all(value, "tensor", split_axis=0, concat_axis=0, tiled=True)


def full_weight(shard, axis):
    parts = lax.all_gather(shard, "tensor", axis=0, tiled=False)
    return lax.all_gather(parts, "dp", axis=axis + 1, tiled=True)


def reduce_weight(parts, axis):
    mine = lax.psum_scatter(parts, "dp", scatter_dimension=axis + 1, tiled=True)
    return lax.psum_scatter(mine, "tensor", scatter_dimension=0, tiled=False).astype(jnp.float32)


def contract_first(left, right):
    return low_dot(left, right, ((0,), (0,)))


def contract_last(left, right):
    return low_dot(left, right, ((1,), (1,)))


def split_columns(value):
    size = lax.axis_size("dp")
    rows, cols = value.shape
    return value.reshape(rows, size, cols // size).transpose(1, 0, 2).reshape(size, -1)


def reduce_small(values):
    size = lax.axis_size("dp")
    packed = jnp.concatenate([split_columns(value) for value in values], axis=1)
    length = packed.shape[1]
    rows = -(-length // 1024) * 8
    packed = jnp.pad(packed, ((0, 0), (0, rows * 128 - length))).reshape(size, rows, 128)
    mine = lax.psum_scatter(packed, "dp", scatter_dimension=0, tiled=False)
    mine = sum_tensor(mine).reshape(-1)
    result, first = [], 0
    for value in values:
        count = value.shape[0] * value.shape[1] // size
        result.append(mine[first : first + count].reshape(value.shape[0], -1))
        first += count
    return result


def gather_small(values):
    size = lax.axis_size("dp")
    packed = jnp.concatenate([value.reshape(-1) for value in values])
    length = packed.shape[0]
    rows = -(-length // 2048) * 16
    packed = jnp.pad(packed, (0, rows * 128 - length)).reshape(rows, 128)
    every = lax.all_gather(packed, "dp", axis=0, tiled=False).reshape(size, -1)
    result, first = [], 0
    for value in values:
        count = value.size
        block = every[:, first : first + count].reshape(size, value.shape[0], -1)
        result.append(block.transpose(1, 0, 2).reshape(value.shape[0], -1))
        first += count
    return result


def body(
    streams,
    prior,
    seg_ids,
    positions,
    w_qk,
    w_value,
    w_out,
    w_up,
    w_down,
    norm_gain,
    norm_bias,
    mix_in,
    mix_out,
    mix_bias,
    d_streams,
):
    rows_dev = streams.shape[1]
    bf16 = jnp.bfloat16
    place = lax.axis_index("tensor")
    gains, shifts, mixin_cols, mixout_all, mixbias_all = gather_small(
        [norm_gain, norm_bias, mix_in.T, mix_out, mix_bias[None]]
    )
    gains, shifts = gains.astype(jnp.float32), shifts.astype(jnp.float32)
    mixout_all, mixbias_all = mixout_all.astype(jnp.float32), mixbias_all.astype(jnp.float32)
    query_full = full_weight(w_qk[0], 0)
    key_full = full_weight(w_qk[1], 0)
    value_full = full_weight(w_value, 0)
    out_full = full_weight(w_out, 1)
    up_all = lax.all_gather(w_up, "dp", axis=0, tiled=True)
    down_all = lax.all_gather(w_down, "dp", axis=1, tiled=True)

    tables = rotary_tables(positions)
    own_tables = [lax.dynamic_slice_in_dim(t, place * rows_dev, rows_dev) for t in tables]
    normed = norm_streams(streams, 3, gains[:3], shifts[:3])
    query = exchange(project(normed[0], query_full, own_tables, name="query"))
    key = exchange(project(normed[1], key_full, own_tables, name="key"))
    value = exchange(project(normed[2], value_full, name="value"))
    heads_shape = (value.shape[0] * value.shape[1], value.shape[2])
    query, key, value = (x.reshape(heads_shape) for x in (query, key, value))
    attended, logs = attend(query, key, value, positions, seg_ids)
    attended_rows = exchange(attended.reshape(-1, rows_dev, heads_shape[1]))
    attn_result = join(attended_rows, out_full, name="attn_out")
    mid, mlp_input = middle(attn_result, streams, gains[3], shifts[3])

    mlp_rows = spread_rows(mlp_input)
    hidden, slopes, parts = [], [], []
    for rows in mlp_rows:
        acts, slope = gelu_pair(low_dot(rows, up_all, ((1,), (0,))))
        hidden.append(acts.astype(bf16))
        slopes.append(slope.astype(bf16))
        parts.append(low_dot(hidden[-1], down_all, ((1,), (0,))).astype(bf16))
    parts = collect_rows(parts)
    (
        new_streams,
        grad_prior,
        grad_layer,
        grad_layer_low,
        grad_mix_in,
        grad_mix_out,
        grad_mix_bias,
        gain_four,
        shift_four,
    ) = mixer(
        mid, parts, prior, d_streams, gains[4], shifts[4], mixin_cols, mixout_all, mixbias_all[0]
    )

    grad_rows = spread_rows(grad_layer_low)
    grad_pre, parts = [], []
    for rows, slope in zip(grad_rows, slopes):
        grad_hidden = contract_last(rows, down_all)
        grad_pre.append((grad_hidden * slope.astype(jnp.float32)).astype(bf16))
        parts.append(contract_last(grad_pre[-1], up_all).astype(bf16))
    parts = collect_rows(parts)
    grad_w_down = contract_first(jnp.concatenate(hidden), jnp.concatenate(grad_rows)).astype(bf16)
    grad_w_up = contract_first(jnp.concatenate(mlp_rows), jnp.concatenate(grad_pre)).astype(bf16)
    grad_mid, gain_three, shift_three = middle_back(mid, grad_layer, parts, gains[3])

    grad_attended = exchange(project(grad_mid, out_full, swap=True, name="attn_out_back"))
    grad_query, grad_key, grad_value = attend_back(
        query,
        key,
        value,
        attended,
        grad_attended.reshape(heads_shape),
        logs,
        positions,
        seg_ids,
        *tables,
    )
    grad_w_out = weight_grad(grad_mid, attended_rows, swap=True, name="grad_w_out")
    back, grads = [], []
    for index, (grad, full) in enumerate(
        ((grad_query, query_full), (grad_key, key_full), (grad_value, value_full))
    ):
        rows = exchange(grad.reshape(-1, rows_dev, heads_shape[1]))
        grads.append(weight_grad(normed[index], rows, name="grad_w_in"))
        back.append(join(rows, full, swap=True, name="attn_in_back"))
    grad_streams, gain_first, shift_first = streams_back(streams, *back, grad_mid, gains[:3])

    shard_up = lax.psum_scatter(grad_w_up, "dp", scatter_dimension=0, tiled=True)
    shard_down = lax.psum_scatter(grad_w_down, "dp", scatter_dimension=1, tiled=True)
    shard_out = reduce_weight(grad_w_out, 1)
    shard_query, shard_key, shard_value = (reduce_weight(grad, 0) for grad in grads)
    late_gain, late_shift, total_mix_in, total_mix_out, total_mix_bias = reduce_small(
        [
            jnp.concatenate([gain_three, gain_four]),
            jnp.concatenate([shift_three, shift_four]),
            grad_mix_in,
            grad_mix_out,
            grad_mix_bias,
        ]
    )
    early_gain, early_shift = reduce_small([gain_first[:, 0], shift_first[:, 0]])
    return (
        new_streams,
        grad_streams,
        grad_prior,
        jnp.stack([shard_query, shard_key]),
        shard_value,
        shard_out,
        shard_up.astype(jnp.float32),
        shard_down.astype(jnp.float32),
        jnp.concatenate([early_gain, late_gain]),
        jnp.concatenate([early_shift, late_shift]),
        total_mix_in.T,
        total_mix_out,
        total_mix_bias[0],
    )


def solution(mesh):
    in_specs = (
        P(None, ("dp", "tensor"), None),
        P(None, ("dp", "tensor"), None),
        P("dp"),
        P("dp"),
        P(None, "dp", "tensor"),
        P("dp", "tensor"),
        P("tensor", "dp"),
        P("dp", "tensor"),
        P("tensor", "dp"),
        P(None, "dp"),
        P(None, "dp"),
        P("dp", None),
        P(None, "dp"),
        P("dp"),
        P(None, ("dp", "tensor"), None),
    )
    out_specs = (
        P(None, ("dp", "tensor"), None),
        P(None, ("dp", "tensor"), None),
        P(None, ("dp", "tensor"), None),
        P(None, "dp", "tensor"),
        P("dp", "tensor"),
        P("tensor", "dp"),
        P("dp", "tensor"),
        P("tensor", "dp"),
        P(None, "dp"),
        P(None, "dp"),
        P("dp", None),
        P(None, "dp"),
        P("dp"),
    )
    return jax.shard_map(body, mesh=mesh, in_specs=in_specs, out_specs=out_specs, check_vma=False)
```

time: 2560 us -> 1820 us (0.71)
  matrix products: 921 us -> 211 us
  Pallas kernels: 0 us -> 336 us
  other arithmetic: 322 us -> 32 us
  local copies, waits for them, and re-layouts: 186 us -> 60.4 us
  starting transfers between devices: 15.5 us -> 44.8 us
  waiting for transfers between devices: 970 us -> 999 us
    dot_general x62 -> x22, matrix products: 921 us -> 211 us  [low_dot(): lax.dot_general(a, b, (dims, ((), ())), preferred_element_type=jnp.float32)]
    pallas_call x0 -> x19, Pallas kernels: none -> 336 us  [the longest x1 71 us: attend_back(): pl.pallas_call(functools.partial(attend_back_kernel, block), grid=grid, i...]
    all_gather x14 -> x10, waiting for transfers between devices: 583 us -> 324 us  [the longest x4 174 us: full_weight(): return lax.all_gather(parts, 'dp', axis=axis + 1, tiled=True)]
    ppermute x0 -> x20, waiting for transfers between devices: none -> 209 us  [hop(): return lax.ppermute(value, 'tensor', [(i, i ^ mask) for i in range(size)])]
    convert_element_type x20 -> x11, other arithmetic: 170 us -> 11 us  [the longest x2 3.58 us: reduce_weight(): lax.psum_scatter(mine, 'tensor', scatter_dimension=0, tiled=False)]
    unnamed x23 -> x26, waiting for transfers between devices: 6.12 us -> 121 us
    reduce_sum x14 -> x0, other arithmetic: 101 us -> none  [the longest x5 55.4 us: forward_block(): jnp.sum(jnp.exp(scores - row_max), axis=-1, keepdims=True)]
    reduce_scatter x7 -> x8, waiting for transfers between devices: 334 us -> 268 us  [the longest x1 87.4 us: body(): lax.psum_scatter(grad_w_down, 'dp', scatter_dimension=1, tiled=True)]
  transfers between devices with their start and end apart: 26 -> 47, of which waited for: 17 -> 33; matrix products, arithmetic and copies ran while one was open for 44% -> 14% of each run, Pallas kernels for 0% -> 15%
where the time goes in v1:
time: 1820 us; the launch traced here: 1810 us
  waiting for transfers between devices  999 us (55%)
  Pallas kernels  336 us (18%)
  matrix products  211 us (12%)
  blocking collectives  113 us (6%)
  local copies, waits for them, and re-layouts  60.4 us (3%)
  starting transfers between devices  44.8 us (2%)
  other arithmetic  32 us (2%)
    dot_general x22, matrix products, low_dot(): lax.dot_general(a, b, (dims, ((), ())), preferred_element_type=jnp.float32)  211 us
    ppermute x20, waiting for transfers between devices, hop(): return lax.ppermute(value, 'tensor', [(i, i ^ mask) for i in range(size)])  209 us
    all_gather x4, waiting for transfers between devices, full_weight(): return lax.all_gather(parts, 'dp', axis=axis + 1, tiled=True)  174 us
    unnamed x26, waiting for transfers between devices  121 us
    all_gather x4, waiting for transfers between devices, full_weight(): parts = lax.all_gather(shard, 'tensor', axis=0, tiled=False)  114 us
    all_to_all x3, blocking collectives, exchange(): lax.all_to_all(value, 'tensor', split_axis=0, concat_axis=0, tiled=True)  98.5 us
    reduce_scatter x1, waiting for transfers between devices, body(): lax.psum_scatter(grad_w_down, 'dp', scatter_dimension=1, tiled=True)  87.4 us
    reduce_scatter x1, waiting for transfers between devices, body(): lax.psum_scatter(grad_w_up, 'dp', scatter_dimension=0, tiled=True)  79.1 us
  transfers between devices with their start and end apart: 47, of which 33 were waited for; matrix products, arithmetic and copies ran while one was open for 14% of the time, Pallas kernels for 15%

profile of v1, /device:TPU:0, one launch (start us, length us, event | category | flops | bytes accessed | tf_op | source)
XLA Modules:
  0.0 1810.7 jit_solution(18126039581195393537)
XLA Ops:
  11.2 28.4 %all-gather.13.cloned.1.call-done = bf16[4,256,512]{2,1,0:T(8,128)(2,1)} async-done(((bf16[1,256,512]{2,1,0:T(8,128)(2,1)}), bf16[4,256,512]{2,1,0:T(8,128)(2,1)}) %all-gather.13.cloned.1.call-update) | async-done | bytes 1048592 | tf_op jit(solution)/shard_map/all_gather | solution.py:483
  39.8 28.8 %all-gather.17.cloned.1.call-done = bf16[4,256,512]{2,1,0:T(8,128)(2,1)} async-done(((bf16[1,256,512]{2,1,0:T(8,128)(2,1)}), bf16[4,256,512]{2,1,0:T(8,128)(2,1)}) %all-gather.17.cloned.1.call-update) | async-done | bytes 1048592 | tf_op jit(solution)/shard_map/all_gather | solution.py:483
  167.6 41.3 %all-gather.15.cloned.1.call-done.w_ref = bf16[4,2048,512]{2,1,0:T(8,128)(2,1)} async-done(((bf16[4,256,512]{2,1,0:T(8,128)(2,1)}), bf16[4,2048,512]{2,1,0:T(8,128)(2,1)}) %all-gather.15.cloned.1.call-update) | async-done | bytes 8388624 | tf_op jit(solution)/shard_map/all_gather | solution.py:484
  223.8 66.9 %all-gather.19.cloned.1.call-done.w_ref = bf16[4,2048,512]{2,1,0:T(8,128)(2,1)} async-done(((bf16[4,256,512]{2,1,0:T(8,128)(2,1)}), bf16[4,2048,512]{2,1,0:T(8,128)(2,1)}) %all-gather.19.cloned.1.call-update) | async-done | bytes 8388624 | tf_op jit(solution)/shard_map/all_gather | solution.py:484
  307.5 65.4 %all-gather.21.cloned.1.call-done.w_ref = bf16[4,2048,512]{2,1,0:T(8,128)(2,1)} async-done(((bf16[4,256,512]{2,1,0:T(8,128)(2,1)}), bf16[4,2048,512]{2,1,0:T(8,128)(2,1)}) %all-gather.21.cloned.1.call-update) | async-done | bytes 8388624 | tf_op jit(solution)/shard_map/all_gather | solution.py:484
  419.4 50.3 %attend.1 = (bf16[2560,512]{1,0:T(8,128)(2,1)}, f32[4,1,2560]{2,1,0:T(1,128)}) custom-call(bf16[2560,512]{1,0:T(8,128)(2,1)} %bitcast.157, bf16[2560,512]{1,0:T(8,128)(2,1)} %bitcast.9.k_ref, bf16[2560,512]{1,0:T(8,128)(2,1)} %bitcast.159, s32[2560,1]{1,0:T(8,128)} %broadcast_in_dim.31.pc_ref, s32[2560,1]{1,0:T(8,128)} %broadcast_in_dim.32.sc_ref, ...), custom_call_target="tpu_custom_call" | custom-call | flops 30000001024 | bytes 10485760 | tf_op jit(solution)/shard_map/attend/pallas_call | solution.py:66
  474.6 29.1 %all-to-all-done.3.a_ref = bf16[4,640,512]{2,1,0:T(8,128)(2,1)S(1)} async-done(((bf16[4,640,512]{2,1,0:T(8,128)(2,1)}), bf16[4,640,512]{2,1,0:T(8,128)(2,1)S(1)}, u32[]{:S(2)}, u32[]{:S(2)}) %all-to-all-start.3) | async-done | bytes 2621472 | tf_op jit(solution)/shard_map/all_to_all | solution.py:479
  548.9 32.6 %collective-permute-done = bf16[640,2048]{1,0:T(8,128)(2,1)S(1)} collective-permute-done((bf16[640,2048]{1,0:T(8,128)(2,1)}, bf16[640,2048]{1,0:T(8,128)(2,1)S(1)}, u32[]{:S(2)}, u32[]{:S(2)}) %collective-permute-start) | collective-permute-done | bytes 2621472 | tf_op jit(solution)/shard_map/ppermute | solution.py:441
  708.7 39.1 %collective-permute-done.4.left_ref = bf16[640,2048]{1,0:T(8,128)(2,1)S(1)} collective-permute-done((bf16[640,2048]{1,0:T(8,128)(2,1)}, bf16[640,2048]{1,0:T(8,128)(2,1)S(1)}, u32[]{:S(2)}, u32[]{:S(2)}) %collective-permute-start.4) | collective-permute-done | bytes 2621472 | tf_op jit(solution)/shard_map/ppermute | solution.py:441
  751.9 34.0 %mixer.1 = (bf16[4,640,2048]{2,1,0:T(8,128)(2,1)}, bf16[3,640,2048]{2,1,0:T(8,128)(2,1)}, f32[640,2048]{1,0:T(8,128)}, bf16[640,2048]{1,0:T(8,128)(2,1)}, f32[16...) custom-call(f32[640,2048]{1,0:T(8,128)} %get-tuple-element.36.mid_ref, ...), custom_call_target="tpu_custom_call" | custom-call | flops 1000000 | bytes 60000000 | tf_op jit(solution)/shard_map/mixer/pallas_call | solution.py:263
  800.3 42.8 %collective-permute-done.8 = bf16[640,2048]{1,0:T(8,128)(2,1)S(1)} collective-permute-done((bf16[640,2048]{1,0:T(8,128)(2,1)}, bf16[640,2048]{1,0:T(8,128)(2,1)S(1)}, u32[]{:S(2)}, u32[]{:S(2)}) %collective-permute-start.8) | collective-permute-done | bytes 2621472 | tf_op jit(solution)/shard_map/ppermute | solution.py:441
  941.1 43.2 %collective-permute-done.12.left_ref = bf16[640,2048]{1,0:T(8,128)(2,1)S(1)} collective-permute-done((bf16[640,2048]{1,0:T(8,128)(2,1)S(1)}, bf16[640,2048]{1,0:T(8,128)(2,1)S(1)}, u32[]{:S(2)}, u32[]{:S(2)}) %collective-permute-start.12) | collective-permute-done | bytes 2621472 | tf_op jit(solution)/shard_map/ppermute | solution.py:441
  1051.1 71.0 %attend_back.1 = (bf16[2560,512]{1,0:T(8,128)(2,1)}, bf16[2560,512]{1,0:T(8,128)(2,1)}, bf16[2560,512]{1,0:T(8,128)(2,1)}) custom-call(bf16[2560,512]{1,0:T(8,128)(2,1)} %bitcast.158, bf16[2560,512]{1,0:T(8,128)(2,1)} %bitcast.9.k_ref, bf16[2560,512]{1,0:T(8,128)(2,1)} %bitcast.160, bf16[2560,512]{1,0:T(8,128)(2,1)} %get-tuple-element.35.o_ref, ...), custom_call_target="tpu_custom_call" | custom-call | flops 80000000000 | bytes 20971520 | tf_op jit(solution)/shard_map/attend_back/pallas_call | solution.py:140
  1122.1 35.0 %all_to_all.40.a_ref = bf16[4,640,512]{2,1,0:T(8,128)(2,1)} all-to-all(bf16[4,640,512]{2,1,0:T(8,128)(2,1)} %bitcast.164), channel_id=1, replica_groups=mesh['dp'=8,'tensor'=4] {'tensor'}, dimensions={0} | all-to-all | bytes 5242880 | tf_op jit(solution)/shard_map/all_to_all | solution.py:479
  1170.0 32.4 %all_to_all.41.a_ref = bf16[4,640,512]{2,1,0:T(8,128)(2,1)} all-to-all(bf16[4,640,512]{2,1,0:T(8,128)(2,1)S(1)} %bitcast.163), channel_id=1, replica_groups=mesh['dp'=8,'tensor'=4] {'tensor'}, dimensions={0} | all-to-all | bytes 5242880 | tf_op jit(solution)/shard_map/all_to_all | solution.py:479
  1215.5 31.1 %all_to_all.42.a_ref = bf16[4,640,512]{2,1,0:T(8,128)(2,1)} all-to-all(bf16[4,640,512]{2,1,0:T(8,128)(2,1)S(1)} %bitcast.162), channel_id=1, replica_groups=mesh['dp'=8,'tensor'=4] {'tensor'}, dimensions={0} | all-to-all | bytes 5242880 | tf_op jit(solution)/shard_map/all_to_all | solution.py:479
  1327.8 29.0 %convolution_convert_fusion.1 = bf16[2048,2048]{1,0:T(8,128)(2,1)} fusion(bf16[2560,2048]{1,0:T(8,128)(2,1)} %constant_dynamic-update-slice_fusion, bf16[2560,2048]{1,0:T(8,128)(2,1)} %get-tuple-element.118), kind=kOutput, calls=%fused_computation.4 | convolution fusion | flops 21479030784 | bytes 29360128 | tf_op jit(solution)/shard_map/dot_general | solution.py:166
  1392.3 44.2 %reduce-scatter.21.cloned.1.call-done = bf16[4,256,512]{2,1,0:T(8,128)(2,1)} async-done(((bf16[4,2048,512]{2,1,0:T(8,128)(2,1)}), bf16[4,256,512]{2,1,0:T(8,128)(2,1)}) %reduce-scatter.21.cloned.1.call-update) | async-done | bytes 1048592 | tf_op jit(solution)/shard_map/reduce_scatter | solution.py:488
  1436.4 31.8 %reduce-scatter.35.cloned.1.call-done = f32[1,48,128]{2,1,0:T(8,128)} async-done(((f32[8,48,128]{2,1,0:T(8,128)}), f32[1,48,128]{2,1,0:T(8,128)}) %reduce-scatter.35.cloned.1.call-update) | async-done | bytes 24592 | tf_op jit(solution)/shard_map/reduce_scatter | solution.py:512
  1510.3 79.1 %reduce-scatter.29.cloned.1.call-done = bf16[256,2048]{1,0:T(8,128)(2,1)} async-done(((bf16[2048,2048]{1,0:T(8,128)(2,1)}), bf16[256,2048]{1,0:T(8,128)(2,1)}) %reduce-scatter.29.cloned.1.call-update) | async-done | bytes 1048592 | tf_op jit(solution)/shard_map/reduce_scatter | solution.py:638
  1592.3 87.4 %reduce-scatter.31.cloned.1.call-done = bf16[2048,256]{1,0:T(8,128)(2,1)} async-done(((bf16[2048,2048]{1,0:T(8,128)(2,1)}), bf16[2048,256]{1,0:T(8,128)(2,1)}) %reduce-scatter.31.cloned.1.call-update) | async-done | bytes 1048592 | tf_op jit(solution)/shard_map/reduce_scatter | solution.py:639
  1710.8 28.9 %reduce-scatter.41.cloned.1.call-done = bf16[1,256,512]{2,1,0:T(8,128)(2,1)} async-done(((bf16[4,256,512]{2,1,0:T(8,128)(2,1)}), bf16[1,256,512]{2,1,0:T(8,128)(2,1)}) %reduce-scatter.41.cloned.1.call-update) | async-done | bytes 262160
  1741.5 29.1 %reduce-scatter.39.cloned.1.call-done = bf16[1,256,512]{2,1,0:T(8,128)(2,1)} async-done(((bf16[4,256,512]{2,1,0:T(8,128)(2,1)}), bf16[1,256,512]{2,1,0:T(8,128)(2,1)}) %reduce-scatter.39.cloned.1.call-update) | async-done | bytes 262160
  1770.5 30.9 %reduce-scatter.37.cloned.1.call-done = bf16[1,256,512]{2,1,0:T(8,128)(2,1)} async-done(((bf16[4,256,512]{2,1,0:T(8,128)(2,1)}), bf16[1,256,512]{2,1,0:T(8,128)(2,1)}) %reduce-scatter.37.cloned.1.call-update) | async-done | bytes 262160
  (357 shorter events, 763.3 us)
Async XLA Ops:
  9.1 59.5 %all-gather.17.cloned.1.call-start = ((), (), s32[]{:S(2)}) async-start(), calls=%async_computation.22 | async-start | bytes 1310720 | tf_op jit(solution)/shard_map/all_gather | solution.py:483
  9.9 87.1 %all-gather.29.cloned.1.call-start = ((), (), s32[]{:S(2)}) async-start(), calls=%async_computation.36 | async-start | bytes 1310720 | tf_op jit(solution)/shard_map/all_gather | solution.py:483
  10.6 114.6 %all-gather.31.cloned.1.call-start = ((), (), s32[]{:S(2)}) async-start(), calls=%async_computation.37 | async-start | bytes 1310720 | tf_op jit(solution)/shard_map/all_gather | solution.py:483
  11.2 197.7 %all-gather.15.cloned.1.call-start = ((), (), s32[]{:S(2)}) async-start(), calls=%async_computation.21 | async-start | bytes 9437184 | tf_op jit(solution)/shard_map/all_gather | solution.py:484
  39.7 251.0 %all-gather.19.cloned.1.call-start = ((), (), s32[]{:S(2)}) async-start(), calls=%async_computation.23 | async-start | bytes 9437184 | tf_op jit(solution)/shard_map/all_gather | solution.py:484
  68.6 304.3 %all-gather.21.cloned.1.call-start = ((), (), s32[]{:S(2)}) async-start(), calls=%async_computation.24 | async-start | bytes 9437184 | tf_op jit(solution)/shard_map/all_gather | solution.py:484
  97.0 377.6 %all-gather.23.cloned.1.call-start = ((), (), s32[]{:S(2)}) async-start(), calls=%async_computation.25 | async-start | bytes 9437184 | tf_op jit(solution)/shard_map/all_gather | solution.py:484
  125.2 412.1 %all-gather.25.cloned.1.call-start = ((), (), s32[]{:S(2)}) async-start(), calls=%async_computation.26 | async-start | bytes 9437184 | tf_op jit(solution)/shard_map/all_gather | solution.py:567
  219.6 81.8 %all-to-all-start = ((bf16[4,640,512]{2,1,0:T(8,128)(2,1)}), bf16[4,640,512]{2,1,0:T(8,128)(2,1)S(1)}, u32[]{:S(2)}, u32[]{:S(2)}) async-start(bf16[4,640,512]{2,1,0:T(8,128)(2,1)} %query.1), calls=%async_computation | async-start | bytes 5242880 | tf_op jit(solution)/shard_map/all_to_all | solution.py:479
  223.2 396.6 %all-gather.27.cloned.1.call-start = ((), (), s32[]{:S(2)}) async-start(), calls=%async_computation.27 | async-start | bytes 9437184 | tf_op jit(solution)/shard_map/all_gather | solution.py:568
  303.0 79.8 %all-to-all-start.1 = ((bf16[4,640,512]{2,1,0:T(8,128)(2,1)}), bf16[4,640,512]{2,1,0:T(8,128)(2,1)}, u32[]{:S(2)}, u32[]{:S(2)}) async-start(bf16[4,640,512]{2,1,0:T(8,128)(2,1)} %key.1), calls=%async_computation.1 | async-start | bytes 5242880 | tf_op jit(solution)/shard_map/all_to_all | solution.py:479
  473.3 916.9 %reduce-scatter.27.cloned.1.call-start = ((), (), s32[]{:S(2)}) async-start(), calls=%async_computation.31 | async-start | bytes 9437184 | tf_op jit(solution)/shard_map/reduce_scatter | solution.py:488
  586.4 60.2 %collective-permute-start.2 = (bf16[320,2048]{1,0:T(8,128)(2,1)}, bf16[320,2048]{1,0:T(8,128)(2,1)}, u32[]{:S(2)}, u32[]{:S(2)}) collective-permute-start(bf16[320,2048]{1,0:T(8,128)(2,1)} %slice.183), channel_id=1, source_target_pairs={{0,1},{1,0},{2,3},{3,2},{4,5},{5,4},{6,7},{7,6},{8,9},{9,8},{10,11... | collective-permute-start | bytes 3932168 | tf_op jit(solution)/shard_map/ppermute | solution.py:441
  1023.9 367.0 %reduce-scatter.25.cloned.1.call-start = ((), (), s32[]{:S(2)}) async-start(), calls=%async_computation.30 | async-start | bytes 9437184 | tf_op jit(solution)/shard_map/reduce_scatter | solution.py:488
  1168.3 223.2 %reduce-scatter.23.cloned.1.call-start = ((), (), s32[]{:S(2)}) async-start(), calls=%async_computation.29 | async-start | bytes 9437184 | tf_op jit(solution)/shard_map/reduce_scatter | solution.py:488
  1213.7 222.7 %reduce-scatter.21.cloned.1.call-start = ((), (), s32[]{:S(2)}) async-start(), calls=%async_computation.28 | async-start | bytes 9437184 | tf_op jit(solution)/shard_map/reduce_scatter | solution.py:488
  1257.9 210.3 %reduce-scatter.35.cloned.1.call-start = ((), (), s32[]{:S(2)}) async-start(), calls=%async_computation.35 | async-start | bytes 221184 | tf_op jit(solution)/shard_map/reduce_scatter | solution.py:512
  1274.8 224.7 %reduce-scatter.33.cloned.1.call-start = ((), (), s32[]{:S(2)}) async-start(), calls=%async_computation.34 | async-start | bytes 73728 | tf_op jit(solution)/shard_map/reduce_scatter | solution.py:512
  1327.8 261.7 %reduce-scatter.29.cloned.1.call-start = ((), (), s32[]{:S(2)}) async-start(), calls=%async_computation.32 | async-start | bytes 9437184 | tf_op jit(solution)/shard_map/reduce_scatter | solution.py:638
  1356.8 322.8 %reduce-scatter.31.cloned.1.call-start = ((), (), s32[]{:S(2)}) async-start(), calls=%async_computation.33 | async-start | bytes 9437184 | tf_op jit(solution)/shard_map/reduce_scatter | solution.py:639
  1390.1 318.8 %reduce-scatter.43.cloned.1.call-start = ((), (), s32[]{:S(2)}) async-start(), calls=%async_computation.41 | async-start | bytes 1310720
  1390.9 348.8 %reduce-scatter.41.cloned.1.call-start = ((), (), s32[]{:S(2)}) async-start(), calls=%async_computation.40 | async-start | bytes 1310720
  1391.5 379.1 %reduce-scatter.39.cloned.1.call-start = ((), (), s32[]{:S(2)}) async-start(), calls=%async_computation.39 | async-start | bytes 1310720
  1392.2 409.2 %reduce-scatter.37.cloned.1.call-start = ((), (), s32[]{:S(2)}) async-start(), calls=%async_computation.38 | async-start | bytes 1310720
  (77 other events, 1740.6 us)
Sparse Core Ops, SparseCore 0:
  10.4 29.2 all-gather.12
  42.1 26.4 all-gather.16
  70.5 26.4 all-gather.28
  98.7 26.4 all-gather.30
  126.7 82.1 all-gather.14
  210.4 80.3 all-gather.18
  292.4 80.5 all-gather.20
  374.5 80.9 all-gather.22
  457.1 80.2 all-gather.24
  538.8 80.9 all-gather.26
  1009.3 87.4 reduce-scatter.26
  1168.4 87.4 reduce-scatter.24
  1258.2 87.9 reduce-scatter.22
  1348.4 88.0 reduce-scatter.20
  1439.1 29.1 reduce-scatter.34
  1470.9 28.5 reduce-scatter.32
  1501.7 87.7 reduce-scatter.28
  1591.6 88.0 reduce-scatter.30
  1682.6 26.3 reduce-scatter.42
  1711.7 27.9 reduce-scatter.40
  1742.6 27.9 reduce-scatter.38
  1773.4 27.9 reduce-scatter.36

commit v2 on v1

--- a/solution.py
+++ b/solution.py
@@ -155,6 +155,9 @@
 ROOT_HALF = math.sqrt(0.5)
 PDF_SCALE = 1.0 / math.sqrt(2.0 * math.pi)
 
+SCALAR = pl.BlockSpec(memory_space=pltpu.SMEM)
+
+
 def gelu_pair(u):
     cdf = 0.5 + 0.5 * lax.erf(u * ROOT_HALF)
     return u * cdf, cdf + u * (PDF_SCALE * jnp.exp(-0.5 * u * u))
@@ -184,21 +187,61 @@
         tile -= 16
     return tile
 
-def norm_kernel(x_ref, gain_ref, shift_ref, n_ref):
+def chunk_starts(core, width, owners):
+    size = width // owners
+    return [
+        (o * size, pl.multiple_of((core ^ (o % 2)) * (width // 2) + (o // 2) * size, size))
+        for o in range(owners)
+    ]
+
+
+def store_halves(ref, value, core, owners):
+    size = value.shape[1] // owners
+    for first, target in chunk_starts(core, value.shape[1], owners):
+        ref[:, pl.ds(target, size)] = value[:, first : first + size]
+
+
+def load_halves(ref, core, owners):
+    width = ref.shape[1]
+    size = width // owners
+    return jnp.concatenate(
+        [ref[:, pl.ds(target, size)] for _, target in chunk_starts(core, width, owners)], axis=1
+    )
+
+
+def norm_kernel(owners, core_ref, x_ref, gain_ref, shift_ref, n_ref):
     xhat, _ = standard(x_ref[0].astype(jnp.float32))
-    n_ref[0] = (xhat * gain_ref[0] + shift_ref[0]).astype(jnp.bfloat16)
-
-def norm_streams(x, count, gains, shifts):
+    value = (xhat * gain_ref[0] + shift_ref[0]).astype(jnp.bfloat16)
+    store_halves(n_ref.at[0], value, core_ref[0], owners)
+
+def norm_streams(x, count, gains, shifts, core, owners):
     rows, width = x.shape[1:]
     tile = row_tile(rows, 128)
     block = pl.BlockSpec((1, tile, width), lambda s, i: (s, i, 0))
     vec = pl.BlockSpec((1, 1, width), lambda s, i: (s, 0, 0))
     return pl.pallas_call(
-        norm_kernel, grid=(count, rows // tile), in_specs=[block, vec, vec], out_specs=block,
+        functools.partial(norm_kernel, owners), grid=(count, rows // tile),
+        in_specs=[SCALAR, block, vec, vec], out_specs=block,
         out_shape=jax.ShapeDtypeStruct((count, rows, width), jnp.bfloat16), name="norm_streams",
-    )(x, gains[:, None, :], shifts[:, None, :])
-
-def mixer_kernel(mid_ref, part_ref, left_ref, right_ref, prior_ref, up_ref, gain_ref, shift_ref,
+    )(core, x, gains[:, None, :], shifts[:, None, :])
+
+def add_parts(part_ref, halves, switch):
+    low = pl.program_id(0) < switch
+    total = part_ref[...].astype(jnp.float32)
+    for first, second in (halves[:2], halves[2:]):
+        total = total + jnp.where(
+            low, first[...].astype(jnp.float32), second[...].astype(jnp.float32)
+        )
+    return total
+
+
+def half_specs(tile, width, switch):
+    first = pl.BlockSpec((tile, width), lambda i: (jnp.minimum(i, switch - 1), 0))
+    second = pl.BlockSpec((tile, width), lambda i: (jnp.maximum(i - switch, 0), 0))
+    return [first, second, first, second]
+
+
+def mixer_kernel(switch, mid_ref, part_ref, xl_ref, xh_ref, yl_ref, yh_ref, prior_ref, up_ref, gain_ref, shift_ref,
                  mixin_ref, mixout_ref, bias_ref,
                  new_ref, gprior_ref, gout_ref, gz_ref, gin_ref, gmo_ref, gmb_ref, gg_ref, gs_ref):
     first = pl.program_id(0) == 0
@@ -206,7 +249,7 @@
     count = up_ref.shape[0]
     tile = mid_ref.shape[0]
     wide = count * sources
-    out = mid_ref[...] + part_ref[...].astype(jnp.float32) + left_ref[...].astype(jnp.float32) + right_ref[...].astype(jnp.float32)
+    out = mid_ref[...] + add_parts(part_ref, (xl_ref, xh_ref, yl_ref, yh_ref), switch)
     xhat, rstd = standard(out)
     gain = gain_ref[...]
     c = (xhat * gain + shift_ref[...]).astype(jnp.bfloat16)
@@ -254,15 +297,16 @@
     rows, width = mid.shape
     hidden = mix_in.shape[0]
     wide = mix_out.shape[1]
-    tile = row_tile(rows, most)
+    tile = row_tile(rows // 2, most)
+    switch = rows // 2 // tile
     flat = pl.BlockSpec((tile, width), lambda i: (i, 0))
     stack = lambda n: pl.BlockSpec((n, tile, width), lambda i: (0, i, 0))
     full = lambda *s: pl.BlockSpec(s, lambda i: (0,) * len(s))
     f32 = jnp.float32
     shape = jax.ShapeDtypeStruct
     return pl.pallas_call(
-        mixer_kernel, grid=(rows // tile,),
-        in_specs=[flat, flat, flat, flat, stack(prior.shape[0]), stack(d_streams.shape[0]),
+        functools.partial(mixer_kernel, switch), grid=(rows // tile,),
+        in_specs=[flat, flat, *half_specs(tile, width, switch), stack(prior.shape[0]), stack(d_streams.shape[0]),
                   full(1, width), full(1, width), full(hidden, width), full(hidden, wide), full(1, wide)],
         out_specs=[stack(d_streams.shape[0]), stack(prior.shape[0]), flat, flat,
                    full(hidden, width), full(hidden, wide), full(1, wide), full(1, width), full(1, width)],
@@ -274,42 +318,44 @@
         name="mixer",
     )(mid, *parts, prior, d_streams, gain[None], shift[None], mix_in, mix_out, mix_bias[None])
 
-def middle_kernel(attn_ref, stream_ref, gain_ref, shift_ref, mid_ref, m_ref):
-    mid = attn_ref[...] + stream_ref[0].astype(jnp.float32)
+def middle_kernel(owners, core_ref, attn_ref, stream_ref, gain_ref, shift_ref, mid_ref, m_ref):
+    mid = load_halves(attn_ref, core_ref[0], owners) + stream_ref[0].astype(jnp.float32)
     mid_ref[...] = mid
     xhat, _ = standard(mid)
     m_ref[...] = (xhat * gain_ref[...] + shift_ref[...]).astype(jnp.bfloat16)
 
-def middle(attn, streams, gain, shift):
+def middle(attn, streams, gain, shift, core, owners):
     rows, width = attn.shape
     tile = row_tile(rows, 128)
     flat = pl.BlockSpec((tile, width), lambda i: (i, 0))
     vec = pl.BlockSpec((1, width), lambda i: (0, 0))
     return pl.pallas_call(
-        middle_kernel, grid=(rows // tile,),
-        in_specs=[flat, pl.BlockSpec((1, tile, width), lambda i: (3, i, 0)), vec, vec],
+        functools.partial(middle_kernel, owners), grid=(rows // tile,),
+        in_specs=[SCALAR, flat, pl.BlockSpec((1, tile, width), lambda i: (3, i, 0)), vec, vec],
         out_specs=[flat, flat],
         out_shape=[jax.ShapeDtypeStruct((rows, width), jnp.float32), jax.ShapeDtypeStruct((rows, width), jnp.bfloat16)],
         name="middle",
-    )(attn, streams, gain[None], shift[None])
-
-def middle_back(mid, gout, parts, gain):
+    )(core, attn, streams, gain[None], shift[None])
+
+def middle_back(mid, gout, parts, gain, core, owners):
     rows, width = mid.shape
-    tile = row_tile(rows, 64)
+    tile = row_tile(rows // 2, 64)
+    switch = rows // 2 // tile
     flat = pl.BlockSpec((tile, width), lambda i: (i, 0))
     vec = pl.BlockSpec((1, width), lambda i: (0, 0))
     shape = jax.ShapeDtypeStruct
     return pl.pallas_call(
-        middle_back_kernel, grid=(rows // tile,),
-        in_specs=[flat] * 5 + [vec], out_specs=[flat, vec, vec],
+        functools.partial(middle_back_kernel, owners, switch), grid=(rows // tile,),
+        in_specs=[SCALAR] + [flat] * 3 + half_specs(tile, width, switch) + [vec], out_specs=[flat, vec, vec],
         out_shape=[shape((rows, width), jnp.bfloat16), shape((1, width), jnp.float32), shape((1, width), jnp.float32)],
         name="middle_back",
-    )(mid, gout, *parts, gain[None])
-
-def middle_back_kernel(mid_ref, gout_ref, part_ref, left_ref, right_ref, gain_ref, low_ref, gg_ref, gs_ref):
+    )(core, mid, gout, *parts, gain[None])
+
+def middle_back_kernel(owners, switch, core_ref, mid_ref, gout_ref, part_ref, xl_ref, xh_ref, yl_ref, yh_ref, gain_ref, low_ref, gg_ref, gs_ref):
     xhat, rstd = standard(mid_ref[...])
-    r = part_ref[...].astype(jnp.float32) + left_ref[...].astype(jnp.float32) + right_ref[...].astype(jnp.float32)
-    low_ref[...] = (gout_ref[...] + pull_standard(xhat, rstd, r * gain_ref[...])).astype(jnp.bfloat16)
+    r = add_parts(part_ref, (xl_ref, xh_ref, yl_ref, yh_ref), switch)
+    value = (gout_ref[...] + pull_standard(xhat, rstd, r * gain_ref[...])).astype(jnp.bfloat16)
+    store_halves(low_ref, value, core_ref[0], owners)
 
     @pl.when(pl.program_id(0) == 0)
     def _():
@@ -319,7 +365,7 @@
     gg_ref[...] += jnp.sum(r * xhat, axis=0, keepdims=True)
     gs_ref[...] += jnp.sum(r, axis=0, keepdims=True)
 
-def streams_back_kernel(x_ref, rq_ref, rk_ref, rv_ref, last_ref, gain_ref, gx_ref, gg_ref, gs_ref):
+def streams_back_kernel(owners, core_ref, x_ref, rq_ref, rk_ref, rv_ref, last_ref, gain_ref, gx_ref, gg_ref, gs_ref):
     @pl.when(pl.program_id(0) == 0)
     def _():
         gg_ref[...] = jnp.zeros_like(gg_ref)
@@ -327,103 +373,158 @@
 
     for s, ref in enumerate((rq_ref, rk_ref, rv_ref)):
         xhat, rstd = standard(x_ref[s].astype(jnp.float32))
-        r = ref[...]
+        r = load_halves(ref, core_ref[0], owners)
         gx_ref[s] = pull_standard(xhat, rstd, r * gain_ref[s]).astype(jnp.bfloat16)
         gg_ref[s] += jnp.sum(r * xhat, axis=0, keepdims=True)
         gs_ref[s] += jnp.sum(r, axis=0, keepdims=True)
-    gx_ref[3] = last_ref[...]
-
-def streams_back(x, rq, rk, rv, last, gains):
+    gx_ref[3] = load_halves(last_ref, core_ref[0], owners)
+
+def streams_back(x, rq, rk, rv, last, gains, core, owners):
     rows, width = rq.shape
     tile = row_tile(rows, 64)
     flat = pl.BlockSpec((tile, width), lambda i: (i, 0))
     three = pl.BlockSpec((3, 1, width), lambda i: (0, 0, 0))
     shape = jax.ShapeDtypeStruct
     return pl.pallas_call(
-        streams_back_kernel, grid=(rows // tile,),
-        in_specs=[pl.BlockSpec((3, tile, width), lambda i: (0, i, 0)), flat, flat, flat, flat, three],
+        functools.partial(streams_back_kernel, owners), grid=(rows // tile,),
+        in_specs=[SCALAR, pl.BlockSpec((3, tile, width), lambda i: (0, i, 0)), flat, flat, flat, flat, three],
         out_specs=[pl.BlockSpec((4, tile, width), lambda i: (0, i, 0)), three, three],
         out_shape=[shape((4, rows, width), jnp.bfloat16), shape((3, 1, width), jnp.float32), shape((3, 1, width), jnp.float32)],
         name="streams_back",
-    )(x, rq, rk, rv, last, gains[:, None, :])
-
-def project_kernel(turn, swap, n_ref, w_ref, *rest):
+    )(core, x, rq, rk, rv, last, gains[:, None, :])
+
+
+def project_kernel(turn, swap, place_ref, n_ref, mine_ref, other_ref, *rest):
+    dims = ((1,), (1 if swap else 0,))
+    half = n_ref.shape[1] // 2
+    y = low_dot(n_ref[:, :half], mine_ref[0], dims) + low_dot(n_ref[:, half:], other_ref[0], dims)
+    o_ref = rest[-1]
     if turn:
-        c_ref, s_ref, o_ref = rest
-    else:
-        (o_ref,) = rest
-    y = low_dot(n_ref[...], w_ref[0], ((1,), (1 if swap else 0,)))
-    if turn:
-        for h in range(y.shape[1] // 128):
-            cols = slice(h * 128, (h + 1) * 128)
+        c_ref, s_ref = rest[:2]
+        for h in range(y.shape[1] // HDIM):
+            cols = slice(h * HDIM, (h + 1) * HDIM)
             part = y[:, cols]
-            o_ref[0, :, cols] = (part * c_ref[...] + pltpu.roll(part, 64, 1) * s_ref[...]).astype(jnp.bfloat16)
+            part = part * c_ref[...] + pltpu.roll(part, HDIM // 2, 1) * s_ref[...]
+            o_ref[0, :, cols] = part.astype(jnp.bfloat16)
     else:
         o_ref[0] = y.astype(jnp.bfloat16)
 
-def project(n, w4, tables=None, swap=False, name="project"):
+
+def project(n, halves, place, tables=(), swap=False, name="project"):
     rows, width = n.shape
-    groups = w4.shape[0]
-    cols = w4.shape[1] if swap else w4.shape[2]
-    specs = [pl.BlockSpec((rows, width), lambda g: (0, 0)), pl.BlockSpec((1,) + w4.shape[1:], lambda g: (g, 0, 0))]
-    args = [n, w4]
-    if tables is not None:
-        specs += [pl.BlockSpec((rows, 128), lambda g: (0, 0))] * 2
-        args += list(tables)
-    return pl.pallas_call(
-        functools.partial(project_kernel, tables is not None, swap), grid=(groups,),
-        in_specs=specs, out_specs=pl.BlockSpec((1, rows, cols), lambda g: (g, 0, 0)),
+    groups = halves[0].shape[0]
+    cols = halves[0].shape[1 if swap else 2]
+    part = pl.BlockSpec((1,) + halves[0].shape[1:], lambda r, p: (r, 0, 0))
+    table = pl.BlockSpec((rows, HDIM), lambda r, p: (0, 0))
+    return pl.pallas_call(
+        functools.partial(project_kernel, bool(tables), swap),
+        grid_spec=pltpu.PrefetchScalarGridSpec(
+            num_scalar_prefetch=1,
+            grid=(groups,),
+            in_specs=[pl.BlockSpec((rows, width), lambda r, p: (0, 0)), part, part]
+            + [table] * len(tables),
+            out_specs=pl.BlockSpec((1, rows, cols), lambda r, p: (p[0] ^ r, 0, 0)),
+        ),
         out_shape=jax.ShapeDtypeStruct((groups, rows, cols), jnp.bfloat16),
-        cost_estimate=pl.CostEstimate(flops=2 * rows * width * cols * groups, bytes_accessed=w4.size * 2, transcendentals=0),
+        cost_estimate=pl.CostEstimate(
+            flops=2 * rows * width * cols * groups,
+            bytes_accessed=2 * width * cols * groups,
+            transcendentals=0,
+        ),
         name=name,
-    )(*args)
-
-def join_kernel(swap, a_ref, w_ref, o_ref):
-    total = None
-    for g in range(a_ref.shape[0]):
-        part = low_dot(a_ref[g], w_ref[g], ((1,), (1 if swap else 0,)))
-        total = part if total is None else total + part
-    o_ref[...] = total
-
-def join(a4, w4, swap=False, name="join"):
-    groups, rows, cols = a4.shape
-    width = w4.shape[1] if swap else w4.shape[2]
+    )(place, n, *halves, *tables)
+
+
+def join_kernel(swap, tiles, place_ref, a_ref, mine_ref, other_ref, o_ref):
+    place = place_ref[0]
+
+    def add_up(w_ref):
+        total = None
+        for r in range(a_ref.shape[0]):
+            part = low_dot(a_ref[place ^ r], w_ref[r], ((1,), (1 if swap else 0,)))
+            total = part if total is None else total + part
+        o_ref[...] = total
+
+    index = pl.program_id(0)
+    pl.when(index < tiles)(lambda: add_up(mine_ref))
+    pl.when(index >= tiles)(lambda: add_up(other_ref))
+
+
+def join(a, halves, place, swap=False, name="join"):
+    groups, rows, cols = a.shape
+    half = halves[0].shape[1 if swap else 2]
     tile = 512
+    tiles = half // tile
+
+    def spec(place_of):
+        if swap:
+            return pl.BlockSpec((groups, tile, cols), lambda i, p: (0, place_of(i), 0))
+        return pl.BlockSpec((groups, cols, tile), lambda i, p: (0, 0, place_of(i)))
+
+    return pl.pallas_call(
+        functools.partial(join_kernel, swap, tiles),
+        grid_spec=pltpu.PrefetchScalarGridSpec(
+            num_scalar_prefetch=1,
+            grid=(2 * tiles,),
+            in_specs=[
+                pl.BlockSpec((groups, rows, cols), lambda i, p: (0, 0, 0)),
+                spec(lambda i: jnp.minimum(i, tiles - 1)),
+                spec(lambda i: jnp.maximum(i - tiles, 0)),
+            ],
+            out_specs=pl.BlockSpec((rows, tile), lambda i, p: (0, i)),
+        ),
+        out_shape=jax.ShapeDtypeStruct((rows, 2 * half), jnp.float32),
+        cost_estimate=pl.CostEstimate(
+            flops=4 * rows * half * cols * groups,
+            bytes_accessed=4 * half * cols * groups,
+            transcendentals=0,
+        ),
+        name=name,
+    )(place, a, *halves)
+
+
+def weight_kernel(swap, place_ref, n_ref, a_ref, mine_ref, other_ref, t_ref):
+    dims = ((1,), (0,))
+    half = n_ref.shape[1] // 2
     if swap:
-        spec = pl.BlockSpec((groups, tile, cols), lambda i: (0, i, 0))
-    else:
-        spec = pl.BlockSpec((groups, cols, tile), lambda i: (0, 0, i))
-    return pl.pallas_call(
-        functools.partial(join_kernel, swap), grid=(width // tile,),
-        in_specs=[pl.BlockSpec((groups, rows, cols), lambda i: (0, 0, 0)), spec],
-        out_specs=pl.BlockSpec((rows, tile), lambda i: (0, i)),
-        out_shape=jax.ShapeDtypeStruct((rows, width), jnp.float32),
-        cost_estimate=pl.CostEstimate(flops=2 * rows * width * cols * groups, bytes_accessed=w4.size * 2, transcendentals=0),
-        name=name,
-    )(a4, w4)
-
-def weight_kernel(swap, n_ref, a_ref, o_ref, t_ref):
-    if swap:
-        o_ref[0] = low_dot(a_ref[0].T, n_ref[...], ((1,), (0,))).astype(jnp.bfloat16)
+        turned = a_ref[0].T
+        mine_ref[0] = low_dot(turned, n_ref[:, :half], dims).astype(jnp.bfloat16)
+        other_ref[0] = low_dot(turned, n_ref[:, half:], dims).astype(jnp.bfloat16)
     else:
         @pl.when(pl.program_id(0) == 0)
         def _():
             t_ref[...] = n_ref[...].T
-        o_ref[0] = low_dot(t_ref[...], a_ref[0], ((1,), (0,))).astype(jnp.bfloat16)
-
-def weight_grad(n, a4, swap=False, name="weight_grad"):
+
+        mine_ref[0] = low_dot(t_ref[:half], a_ref[0], dims).astype(jnp.bfloat16)
+        other_ref[0] = low_dot(t_ref[half:], a_ref[0], dims).astype(jnp.bfloat16)
+
+
+def weight_grad(n, a, place, swap=False, name="weight_grad"):
     rows, width = n.shape
-    groups, _, cols = a4.shape
-    out = (cols, width) if swap else (width, cols)
-    return pl.pallas_call(
-        functools.partial(weight_kernel, swap), grid=(groups,),
-        in_specs=[pl.BlockSpec((rows, width), lambda g: (0, 0)), pl.BlockSpec((1, rows, cols), lambda g: (g, 0, 0))],
-        out_specs=pl.BlockSpec((1,) + out, lambda g: (g, 0, 0)),
-        out_shape=jax.ShapeDtypeStruct((groups,) + out, jnp.bfloat16),
-        scratch_shapes=[pltpu.VMEM((8, 128) if swap else (width, rows), jnp.bfloat16)],
-        cost_estimate=pl.CostEstimate(flops=2 * rows * width * cols * groups, bytes_accessed=groups * width * cols * 2, transcendentals=0),
+    groups, _, cols = a.shape
+    half = width // 2
+    out = (cols, half) if swap else (half, cols)
+    part = pl.BlockSpec((1,) + out, lambda r, p: (r, 0, 0))
+    return pl.pallas_call(
+        functools.partial(weight_kernel, swap),
+        grid_spec=pltpu.PrefetchScalarGridSpec(
+            num_scalar_prefetch=1,
+            grid=(groups,),
+            in_specs=[
+                pl.BlockSpec((rows, width), lambda r, p: (0, 0)),
+                pl.BlockSpec((1, rows, cols), lambda r, p: (p[0] ^ r, 0, 0)),
+            ],
+            out_specs=[part, part],
+            scratch_shapes=[pltpu.VMEM((16, 128) if swap else (width, rows), jnp.bfloat16)],
+        ),
+        out_shape=[jax.ShapeDtypeStruct((groups,) + out, jnp.bfloat16)] * 2,
+        cost_estimate=pl.CostEstimate(
+            flops=2 * rows * width * cols * groups,
+            bytes_accessed=2 * width * cols * groups,
+            transcendentals=0,
+        ),
         name=name,
-    )(n, a4)
+    )(place, n, a)
 
 
 def rotary_tables(position_row):
@@ -449,44 +550,97 @@
     return [own, one, two, hop(one[:half], 2), hop(two[half:], 1)]
 
 
+def add_low(left, right):
+    return (left.astype(jnp.float32) + right.astype(jnp.float32)).astype(jnp.bfloat16)
+
+
 def collect_rows(pieces):
     if lax.axis_size("tensor") != 4:
         total = lax.psum_scatter(pieces[0], "tensor", scatter_dimension=0, tiled=True)
-        zero = jnp.zeros_like(total)
-        return total, zero, zero
+        zero = jnp.zeros_like(total[: total.shape[0] // 2])
+        return total, zero, zero, zero, zero
     own, one, two, far_low, far_high = pieces
     half = own.shape[0] // 2
+    one_low = hop(one[:half], 1)
+    two_high = hop(two[half:], 2)
     low = hop(far_low, 1)
     high = hop(far_high, 2)
-    f32 = jnp.float32
-    two = jnp.concatenate(
-        [(two[:half].astype(f32) + low.astype(f32)).astype(jnp.bfloat16), two[half:]]
-    )
-    one = jnp.concatenate(
-        [one[:half], (one[half:].astype(f32) + high.astype(f32)).astype(jnp.bfloat16)]
-    )
-    return own, hop(one, 1), hop(two, 2)
-
-
-def sum_tensor(value):
-    if lax.axis_size("tensor") != 4:
-        return lax.psum(value, "tensor")
-    value = value + hop(value, 1)
-    return value + hop(value, 2)
+    one_high = hop(add_low(one[half:], high), 1)
+    two_low = hop(add_low(two[:half], low), 2)
+    return own, one_low, one_high, two_low, two_high
+
+
+def sum_all(value):
+    for axis in ("tensor", "dp"):
+        size = lax.axis_size(axis)
+        bit = 1
+        while bit < size:
+            value = value + lax.ppermute(value, axis, [(i, i ^ bit) for i in range(size)])
+            bit *= 2
+    return value
 
 
 def exchange(value):
     return lax.all_to_all(value, "tensor", split_axis=0, concat_axis=0, tiled=True)
 
 
-def full_weight(shard, axis):
-    parts = lax.all_gather(shard, "tensor", axis=0, tiled=False)
-    return lax.all_gather(parts, "dp", axis=axis + 1, tiled=True)
-
-
-def reduce_weight(parts, axis):
-    mine = lax.psum_scatter(parts, "dp", scatter_dimension=axis + 1, tiled=True)
-    return lax.psum_scatter(mine, "tensor", scatter_dimension=0, tiled=False).astype(jnp.float32)
+def reorder(value):
+    size = lax.axis_size("tensor")
+    return value[jnp.arange(size, dtype=jnp.int32) ^ lax.axis_index("tensor")]
+
+
+def return_heads(value):
+    if lax.axis_size("tensor") != 4:
+        return reorder(exchange(value))
+    place = lax.axis_index("tensor")
+    blocks = [lax.dynamic_index_in_dim(value, place ^ r, 0, keepdims=False) for r in range(4)]
+    return jnp.stack([blocks[0]] + [hop(blocks[r], r) for r in (1, 2, 3)])
+
+
+def core_groups():
+    size = lax.axis_size("dp")
+    return [list(range(core, size, 2)) for core in (0, 1)]
+
+
+def core_hop(value):
+    size = lax.axis_size("dp")
+    return lax.ppermute(value, "dp", [(i, i ^ 1) for i in range(size)])
+
+
+def gather_lane(shards, axis):
+    return lax.all_gather(shards, "dp", axis=axis, tiled=True, axis_index_groups=core_groups())
+
+
+def gather_plane(lane):
+    if lax.axis_size("tensor") == 4:
+        own, one, two, low, high = spread_rows(lane)
+        mine = jnp.stack([own, one, two, jnp.concatenate([low, high])])
+    else:
+        mine = reorder(lax.all_gather(lane, "tensor", axis=0, tiled=False))
+    return mine, core_hop(mine)
+
+
+def reduce_core(halves):
+    mine, other = halves
+    return add_low(mine, core_hop(other))
+
+
+def reduce_plane(total):
+    if lax.axis_size("tensor") != 4:
+        return lax.psum_scatter(reorder(total), "tensor", scatter_dimension=0, tiled=False)
+    half = total.shape[1] // 2
+    own, *rest = collect_rows([total[0], total[1], total[2], total[3, :half], total[3, half:]])
+    one_low, one_high, two_low, two_high = (x.astype(jnp.float32) for x in rest)
+    own = own.astype(jnp.float32)
+    return jnp.concatenate(
+        [own[:half] + one_low + two_low, own[half:] + one_high + two_high]
+    ).astype(jnp.bfloat16)
+
+
+def reduce_lane(value, axis):
+    return lax.psum_scatter(
+        value, "dp", scatter_dimension=axis, tiled=True, axis_index_groups=core_groups()
+    ).astype(jnp.float32)
 
 
 def contract_first(left, right):
@@ -509,8 +663,9 @@
     length = packed.shape[1]
     rows = -(-length // 1024) * 8
     packed = jnp.pad(packed, ((0, 0), (0, rows * 128 - length))).reshape(size, rows, 128)
-    mine = lax.psum_scatter(packed, "dp", scatter_dimension=0, tiled=False)
-    mine = sum_tensor(mine).reshape(-1)
+    mine = lax.dynamic_index_in_dim(
+        sum_all(packed), lax.axis_index("dp"), 0, keepdims=False
+    ).reshape(-1)
     result, first = [], 0
     for value in values:
         count = value.shape[0] * value.shape[1] // size
@@ -554,31 +709,37 @@
 ):
     rows_dev = streams.shape[1]
     bf16 = jnp.bfloat16
-    place = lax.axis_index("tensor")
     gains, shifts, mixin_cols, mixout_all, mixbias_all = gather_small(
         [norm_gain, norm_bias, mix_in.T, mix_out, mix_bias[None]]
     )
     gains, shifts = gains.astype(jnp.float32), shifts.astype(jnp.float32)
     mixout_all, mixbias_all = mixout_all.astype(jnp.float32), mixbias_all.astype(jnp.float32)
-    query_full = full_weight(w_qk[0], 0)
-    key_full = full_weight(w_qk[1], 0)
-    value_full = full_weight(w_value, 0)
-    out_full = full_weight(w_out, 1)
+    owners = lax.axis_size("dp")
+    core = (lax.axis_index("dp") % 2).astype(jnp.int32)[None]
+    place = lax.axis_index("tensor").astype(jnp.int32)
+    here, still = place[None], jnp.zeros((1,), jnp.int32)
+    lanes = [gather_lane(w, 0) for w in (w_qk[0], w_qk[1], w_value)]
+    query_full, key_full, value_full = (gather_plane(lane) for lane in lanes)
+    w_out, w_up = lax.optimization_barrier((w_out, w_up, lanes))[:2]
+    lane_out = gather_lane(w_out, 1)
     up_all = lax.all_gather(w_up, "dp", axis=0, tiled=True)
+    w_down = lax.optimization_barrier((w_down, up_all))[0]
     down_all = lax.all_gather(w_down, "dp", axis=1, tiled=True)
 
     tables = rotary_tables(positions)
     own_tables = [lax.dynamic_slice_in_dim(t, place * rows_dev, rows_dev) for t in tables]
-    normed = norm_streams(streams, 3, gains[:3], shifts[:3])
-    query = exchange(project(normed[0], query_full, own_tables, name="query"))
-    key = exchange(project(normed[1], key_full, own_tables, name="key"))
-    value = exchange(project(normed[2], value_full, name="value"))
+    normed = norm_streams(streams, 3, gains[:3], shifts[:3], core, owners)
+    query = exchange(project(normed[0], query_full, here, own_tables, name="query"))
+    key = exchange(project(normed[1], key_full, here, own_tables, name="key"))
+    value = exchange(project(normed[2], value_full, here, name="value"))
     heads_shape = (value.shape[0] * value.shape[1], value.shape[2])
     query, key, value = (x.reshape(heads_shape) for x in (query, key, value))
+    lane_out = lax.optimization_barrier((lane_out, value))[0]
+    out_full = gather_plane(lane_out)
     attended, logs = attend(query, key, value, positions, seg_ids)
     attended_rows = exchange(attended.reshape(-1, rows_dev, heads_shape[1]))
-    attn_result = join(attended_rows, out_full, name="attn_out")
-    mid, mlp_input = middle(attn_result, streams, gains[3], shifts[3])
+    attn_result = join(attended_rows, out_full, here, name="attn_out")
+    mid, mlp_input = middle(attn_result, streams, gains[3], shifts[3], core, owners)
 
     mlp_rows = spread_rows(mlp_input)
     hidden, slopes, parts = [], [], []
@@ -610,10 +771,13 @@
         parts.append(contract_last(grad_pre[-1], up_all).astype(bf16))
     parts = collect_rows(parts)
     grad_w_down = contract_first(jnp.concatenate(hidden), jnp.concatenate(grad_rows)).astype(bf16)
-    grad_w_up = contract_first(jnp.concatenate(mlp_rows), jnp.concatenate(grad_pre)).astype(bf16)
-    grad_mid, gain_three, shift_three = middle_back(mid, grad_layer, parts, gains[3])
-
-    grad_attended = exchange(project(grad_mid, out_full, swap=True, name="attn_out_back"))
+    parts, grad_w_down = lax.optimization_barrier((parts, grad_w_down))
+    shard_down = lax.psum_scatter(grad_w_down, "dp", scatter_dimension=1, tiled=True)
+    grad_mid, gain_three, shift_three = middle_back(
+        mid, grad_layer, parts, gains[3], core, owners
+    )
+
+    grad_attended = exchange(project(grad_mid, out_full, here, swap=True, name="attn_out_back"))
     grad_query, grad_key, grad_value = attend_back(
         query,
         key,
@@ -625,20 +789,27 @@
         seg_ids,
         *tables,
     )
-    grad_w_out = weight_grad(grad_mid, attended_rows, swap=True, name="grad_w_out")
-    back, grads = [], []
-    for index, (grad, full) in enumerate(
-        ((grad_query, query_full), (grad_key, key_full), (grad_value, value_full))
-    ):
-        rows = exchange(grad.reshape(-1, rows_dev, heads_shape[1]))
-        grads.append(weight_grad(normed[index], rows, name="grad_w_in"))
-        back.append(join(rows, full, swap=True, name="attn_in_back"))
-    grad_streams, gain_first, shift_first = streams_back(streams, *back, grad_mid, gains[:3])
-
+    grad_w_out = weight_grad(grad_mid, attended_rows, here, swap=True, name="grad_w_out")
+    plane_out = reduce_plane(reduce_core(grad_w_out))
+    mlp_rows, grad_query = lax.optimization_barrier((mlp_rows, grad_query))
+    grad_w_up = contract_first(jnp.concatenate(mlp_rows), jnp.concatenate(grad_pre)).astype(bf16)
     shard_up = lax.psum_scatter(grad_w_up, "dp", scatter_dimension=0, tiled=True)
-    shard_down = lax.psum_scatter(grad_w_down, "dp", scatter_dimension=1, tiled=True)
-    shard_out = reduce_weight(grad_w_out, 1)
-    shard_query, shard_key, shard_value = (reduce_weight(grad, 0) for grad in grads)
+    rows, totals = [], []
+    for normed_rows, grad in zip(normed, (grad_query, grad_key, grad_value)):
+        rows.append(return_heads(grad.reshape(-1, rows_dev, heads_shape[1])))
+        totals.append(reduce_core(weight_grad(normed_rows, rows[-1], still, name="grad_w_in")))
+    rows, totals = lax.optimization_barrier((rows, totals))
+    back = [
+        join(part, full, still, swap=True, name="attn_in_back")
+        for part, full in zip(rows, (query_full, key_full, value_full))
+    ]
+    grad_streams, gain_first, shift_first = streams_back(
+        streams, *back, grad_mid, gains[:3], core, owners
+    )
+    planes = [reduce_plane(total) for total in totals]
+    planes[0] = lax.optimization_barrier((planes[0], shard_down, shard_up))[0]
+    shard_out = reduce_lane(plane_out, 1)
+    shard_query, shard_key, shard_value = (reduce_lane(plane, 0) for plane in planes)
     late_gain, late_shift, total_mix_in, total_mix_out, total_mix_bias = reduce_small(
         [
             jnp.concatenate([gain_three, gain_four]),

time: 1820 us -> 1470 us (0.81)
  waiting for transfers between devices: 999 us -> 611 us
  blocking collectives: 113 us -> 16.5 us
  starting transfers between devices: 44.8 us -> 113 us
  other arithmetic: 32 us -> 87.3 us
    ppermute x20 -> x69, waiting for transfers between devices: 209 us -> 429 us  [hop(): return lax.ppermute(value, 'tensor', [(i, i ^ mask) for i in range(size)])]
    all_gather x8 -> x4, waiting for transfers between devices: 287 us -> 88.8 us  [gather_lane(): lax.all_gather(shards, 'dp', axis=axis, tiled=True, axis_index_groups=cor...]
    unnamed x26 -> x12, waiting for transfers between devices: 121 us -> 2.54 us
    reduce_scatter x6 -> x4, waiting for transfers between devices: 101 us -> 0.01 us  [reduce_lane(): lax.psum_scatter(value, 'dp', scatter_dimension=axis, tiled=True, axis_in...]
    all_to_all x3 -> x0, blocking collectives: 98.5 us -> none  [exchange(): lax.all_to_all(value, 'tensor', split_axis=0, concat_axis=0, tiled=True)]
    reduce_scatter x1, waiting for transfers between devices: 87.4 us -> 0.01 us  [body(): lax.psum_scatter(grad_w_down, 'dp', scatter_dimension=1, tiled=True)]
    reduce_scatter x1, waiting for transfers between devices: 79.1 us -> 0.01 us  [body(): lax.psum_scatter(grad_w_up, 'dp', scatter_dimension=0, tiled=True)]
    ppermute x20 -> x69, starting transfers between devices: 23.2 us -> 78.3 us  [hop(): return lax.ppermute(value, 'tensor', [(i, i ^ mask) for i in range(size)])]
  transfers between devices with their start and end apart: 47 -> 104, of which waited for: 33 -> 53; matrix products, arithmetic and copies ran while one was open for 14% -> 23% of each run, Pallas kernels for 15% -> 21%
where the time goes in v2:
time: 1470 us; the launch traced here: 1460 us
  waiting for transfers between devices  611 us (42%)
  Pallas kernels  339 us (23%)
  matrix products  217 us (15%)
  starting transfers between devices  113 us (8%)
  other arithmetic  87.3 us (6%)
  local copies, waits for them, and re-layouts  59.9 us (4%)
  blocking collectives  16.5 us (1%)
  between operations  15.6 us (1%)
    ppermute x69, waiting for transfers between devices, hop(): return lax.ppermute(value, 'tensor', [(i, i ^ mask) for i in range(size)])  429 us
    dot_general x22, matrix products, low_dot(): lax.dot_general(a, b, (dims, ((), ())), preferred_element_type=jnp.float32)  217 us
    all_gather x4, waiting for transfers between devices, gather_lane(): lax.all_gather(shards, 'dp', axis=axis, tiled=True, axis_index_groups=cor...  88.8 us
    ppermute x69, starting transfers between devices, hop(): return lax.ppermute(value, 'tensor', [(i, i ^ mask) for i in range(size)])  78.3 us
    all_to_all x5, waiting for transfers between devices, exchange(): lax.all_to_all(value, 'tensor', split_axis=0, concat_axis=0, tiled=True)  76.2 us
    pallas_call x1, Pallas kernels, attend_back(): pl.pallas_call(functools.partial(attend_back_kernel, block), grid=grid, i...  71.2 us
    pallas_call x1, Pallas kernels, attend(): pl.pallas_call(functools.partial(attend_kernel, block), grid=grid, in_spe...  50.5 us
    pallas_call x4, Pallas kernels, weight_grad(): pl.pallas_call(functools.partial(weight_kernel, swap), grid_spec=pltpu.Pr...  43.7 us
  transfers between devices with their start and end apart: 104, of which 53 were waited for; matrix products, arithmetic and copies ran while one was open for 23% of the time, Pallas kernels for 21%

profile of v2, /device:TPU:0, one launch (start us, length us, event | category | flops | bytes accessed | tf_op | source)
XLA Modules:
  0.0 1459.6 jit_solution(2976775002596074195)
XLA Ops:
  10.6 30.2 %all-gather.17.cloned.1.call-done = bf16[1,1024,512]{2,1,0:T(8,128)(2,1)} async-done(((bf16[1,256,512]{2,1,0:T(8,128)(2,1)}), bf16[1,1024,512]{2,1,0:T(8,128)(2,1)}) %all-gather.17.cloned.1.call-update) | async-done | bytes 1048592 | tf_op jit(solution)/shard_map/all_gather | solution.py:611
  40.9 29.5 %all-gather.19.cloned.1.call-done = bf16[1,1024,512]{2,1,0:T(8,128)(2,1)} async-done(((bf16[1,256,512]{2,1,0:T(8,128)(2,1)}), bf16[1,1024,512]{2,1,0:T(8,128)(2,1)}) %all-gather.19.cloned.1.call-update) | async-done | bytes 1048592 | tf_op jit(solution)/shard_map/all_gather | solution.py:611
  70.4 29.0 %all-gather.9.cloned.1.call-done = bf16[1024,512]{1,0:T(8,128)(2,1)} async-done(((bf16[256,512]{1,0:T(8,128)(2,1)}), bf16[1024,512]{1,0:T(8,128)(2,1)}) %all-gather.9.cloned.1.call-update) | async-done | bytes 1048592 | tf_op jit(solution)/shard_map/all_gather | solution.py:611
  103.0 21.7 %collective-permute-done.11 = bf16[1024,512]{1,0:T(8,128)(2,1)S(1)} collective-permute-done((bf16[1024,512]{1,0:T(8,128)(2,1)}, bf16[1024,512]{1,0:T(8,128)(2,1)S(1)}, u32[]{:S(2)}, u32[]{:S(2)}) %collective-permute-start.11) | collective-permute-done | bytes 1048608 | tf_op jit(solution)/shard_map/ppermute | solution.py:542
  143.5 17.4 %collective-permute-done.1 = bf16[1024,512]{1,0:T(8,128)(2,1)S(1)} collective-permute-done((bf16[1024,512]{1,0:T(8,128)(2,1)S(1)}, bf16[1024,512]{1,0:T(8,128)(2,1)S(1)}, u32[]{:S(2)}, u32[]{:S(2)}) %collective-permute-start.1) | collective-permute-done | bytes 1048608 | tf_op jit(solution)/shard_map/ppermute | solution.py:542
  182.6 16.5 %all_gather.21 = bf16[8,64,128]{2,1,0:T(8,128)(2,1)S(1)} all-gather(bf16[1,64,128]{2,1,0:T(8,128)(2,1)S(1)} %pad_bitcast_fusion.1), channel_id=1, replica_groups=mesh['dp'=8,'tensor'=4] {'dp'}, dimensions={0}, use_global_device_ids=true | all-gather | bytes 147456 | tf_op jit(solution)/shard_map/all_gather | solution.py:683
  203.1 14.5 norm_streams.1
  291.5 18.0 %all-to-all-done = bf16[4,640,512]{2,1,0:T(8,128)(2,1)} async-done(((bf16[4,640,512]{2,1,0:T(8,128)(2,1)}), bf16[4,640,512]{2,1,0:T(8,128)(2,1)}, u32[]{:S(2)}, u32[]{:S(2)}) %all-to-all-start) | async-done | bytes 2621472 | tf_op jit(solution)/shard_map/all_to_all | solution.py:584
  313.8 19.2 %collective-permute-done.16 = bf16[512,1024]{1,0:T(8,128)(2,1)} collective-permute-done((bf16[512,1024]{1,0:T(8,128)(2,1)}, bf16[512,1024]{1,0:T(8,128)(2,1)}, u32[]{:S(2)}, u32[]{:S(2)}) %collective-permute-start.16) | collective-permute-done | bytes 1048608 | tf_op jit(solution)/shard_map/ppermute | solution.py:542
  341.5 28.0 %collective-permute-done.18 = bf16[256,1024]{1,0:T(8,128)(2,1)S(1)} collective-permute-done((bf16[256,1024]{1,0:T(8,128)(2,1)S(1)}, bf16[256,1024]{1,0:T(8,128)(2,1)S(1)}, u32[]{:S(2)}, u32[]{:S(2)}) %collective-permute-start.18) | collective-permute-done | bytes 524320 | tf_op jit(solution)/shard_map/ppermute | solution.py:542
  374.5 50.5 %attend.1 = (bf16[2560,512]{1,0:T(8,128)(2,1)}, f32[4,1,2560]{2,1,0:T(1,128)}) custom-call(bf16[2560,512]{1,0:T(8,128)(2,1)} %bitcast.13.q_ref, bf16[2560,512]{1,0:T(8,128)(2,1)} %bitcast.325, bf16[2560,512]{1,0:T(8,128)(2,1)} %bitcast.323, s32[2560,1]{1,0:T(8,128)} %broadcast_in_dim.39.pc_ref, s32[2560,1]{1,0:T(8,128)} %broadcast_in_dim.40.sc_ref, ...), custom_call_target="tpu_custom_call" | custom-call | flops 30000001024 | bytes 10485760 | tf_op jit(solution)/shard_map/attend/pallas_call | solution.py:66
  430.3 29.7 %all-to-all-done.3.a_ref = bf16[4,640,512]{2,1,0:T(8,128)(2,1)S(1)} async-done(((bf16[4,640,512]{2,1,0:T(8,128)(2,1)}), bf16[4,640,512]{2,1,0:T(8,128)(2,1)S(1)}, u32[]{:S(2)}, u32[]{:S(2)}) %all-to-all-start.3) | async-done | bytes 2621472 | tf_op jit(solution)/shard_map/all_to_all | solution.py:584
  496.9 41.9 %collective-permute-done.20 = bf16[640,2048]{1,0:T(8,128)(2,1)S(1)} collective-permute-done((bf16[640,2048]{1,0:T(8,128)(2,1)}, bf16[640,2048]{1,0:T(8,128)(2,1)S(1)}, u32[]{:S(2)}, u32[]{:S(2)}) %collective-permute-start.20) | collective-permute-done | bytes 2621472 | tf_op jit(solution)/shard_map/ppermute | solution.py:542
  605.1 18.9 %collective-permute-done.24 = bf16[320,2048]{1,0:T(8,128)(2,1)S(1)} collective-permute-done((bf16[320,2048]{1,0:T(8,128)(2,1)S(1)}, bf16[320,2048]{1,0:T(8,128)(2,1)S(1)}, u32[]{:S(2)}, u32[]{:S(2)}) %collective-permute-start.24) | collective-permute-done | bytes 1310752 | tf_op jit(solution)/shard_map/ppermute | solution.py:542
  626.0 21.6 %collective-permute-done.27 = bf16[320,2048]{1,0:T(8,128)(2,1)S(1)} collective-permute-done((bf16[320,2048]{1,0:T(8,128)(2,1)S(1)}, bf16[320,2048]{1,0:T(8,128)(2,1)S(1)}, u32[]{:S(2)}, u32[]{:S(2)}) %collective-permute-start.27) | collective-permute-done | bytes 1310752 | tf_op jit(solution)/shard_map/ppermute | solution.py:542
  656.6 16.3 %collective-permute-done.25.xh_ref = bf16[320,2048]{1,0:T(8,128)(2,1)} collective-permute-done((bf16[320,2048]{1,0:T(8,128)(2,1)S(1)}, bf16[320,2048]{1,0:T(8,128)(2,1)}, u32[]{:S(2)}, u32[]{:S(2)}) %collective-permute-start.25) | collective-permute-done | bytes 1310752 | tf_op jit(solution)/shard_map/ppermute | solution.py:542
  677.4 35.1 %mixer.1 = (bf16[4,640,2048]{2,1,0:T(8,128)(2,1)}, bf16[3,640,2048]{2,1,0:T(8,128)(2,1)}, f32[640,2048]{1,0:T(8,128)}, bf16[640,2048]{1,0:T(8,128)(2,1)}, f32[16...) custom-call(f32[640,2048]{1,0:T(8,128)} %get-tuple-element.69.mid_ref, ...), custom_call_target="tpu_custom_call" | custom-call | flops 1000000 | bytes 60000000 | tf_op jit(solution)/shard_map/mixer/pallas_call | solution.py:307
  740.7 28.1 %collective-permute-done.30 = bf16[640,2048]{1,0:T(8,128)(2,1)S(1)} collective-permute-done((bf16[640,2048]{1,0:T(8,128)(2,1)}, bf16[640,2048]{1,0:T(8,128)(2,1)S(1)}, u32[]{:S(2)}, u32[]{:S(2)}) %collective-permute-start.30) | collective-permute-done | bytes 2621472 | tf_op jit(solution)/shard_map/ppermute | solution.py:542
  829.6 13.9 collective-permute-done.33
  899.6 28.8 %convolution_convert_fusion.1 = bf16[2048,2048]{1,0:T(8,128)(2,1)} fusion(bf16[2560,2048]{1,0:T(8,128)(2,1)} %get-tuple-element.218, bf16[2560,2048]{1,0:T(8,128)(2,1)} %constant_dynamic-update-slice_fusion.5), kind=kOutput, calls=%fused_computation.8 | convolution fusion | flops 21479030784 | bytes 29360128 | tf_op jit(solution)/shard_map/dot_general | solution.py:169
  961.6 15.2 %all-to-all-done.4 = bf16[4,640,512]{2,1,0:T(8,128)(2,1)} async-done(((bf16[4,640,512]{2,1,0:T(8,128)(2,1)}), bf16[4,640,512]{2,1,0:T(8,128)(2,1)}, u32[]{:S(2)}, u32[]{:S(2)}) %all-to-all-start.4) | async-done | bytes 2621472 | tf_op jit(solution)/shard_map/all_to_all | solution.py:584
  976.8 71.2 %attend_back.1 = (bf16[2560,512]{1,0:T(8,128)(2,1)}, bf16[2560,512]{1,0:T(8,128)(2,1)}, bf16[2560,512]{1,0:T(8,128)(2,1)}) custom-call(bf16[2560,512]{1,0:T(8,128)(2,1)} %bitcast.13.q_ref, bf16[2560,512]{1,0:T(8,128)(2,1)} %bitcast.326, bf16[2560,512]{1,0:T(8,128)(2,1)} %bitcast.324, bf16[2560,512]{1,0:T(8,128)(2,1)} %get-tuple-element.66.o_ref, ...), custom_call_target="tpu_custom_call" | custom-call | flops 80000000000 | bytes 20971520 | tf_op jit(solution)/shard_map/attend_back/pallas_call | solution.py:140
  1052.5 26.8 %convolution_convert_fusion = bf16[2048,2048]{1,0:T(8,128)(2,1)} fusion(bf16[2560,2048]{1,0:T(8,128)(2,1)S(1)} %constant_dynamic-update-slice_fusion.10, bf16[2560,2048]{1,0:T(8,128)(2,1)} %get-tuple-element.228), kind=kOutput, calls=%fused_computation.7 | convolution fusion | flops 21479030784 | bytes 29360128 | tf_op jit(solution)/shard_map/dot_general | solution.py:169
  1400.9 19.2 %streams_back.1 = (bf16[4,640,2048]{2,1,0:T(8,128)(2,1)}, f32[3,1,2048]{2,1,0:T(1,128)}, f32[3,1,2048]{2,1,0:T(1,128)}) custom-call(s32[1]{0:T(128)} %bitcast.core_ref, bf16[4,640,2048]{2,1,0:T(8,128)(2,1)} %x_ref.3, f32[640,2048]{1,0:T(8,128)} %attn_in_back.3.rq_ref, f32[640,2048]{1,0:T(8,128)} %attn_in_back.4.rk_ref, f32[640,2048]{1,0:T(8,128)} %attn_in_back.5.rv_ref, ...), custom_call_target="tpu_custom_call" | custom-call | tf_op jit(solution)/shard_map/streams_back/pallas_call | solution.py:388
  (524 shorter events, 802.8 us)
Async XLA Ops:
  9.1 61.3 %all-gather.19.cloned.1.call-start = ((), (), s32[]{:S(2)}) async-start(), calls=%async_computation.22 | async-start | bytes 1310720 | tf_op jit(solution)/shard_map/all_gather | solution.py:611
  9.9 89.5 %all-gather.9.cloned.1.call-start = ((), (), s32[]{:S(2)}) async-start(), calls=%async_computation.11 | async-start | bytes 1310720 | tf_op jit(solution)/shard_map/all_gather | solution.py:611
  10.6 267.0 %all-gather.11.cloned.1.call-start = ((), (), s32[]{:S(2)}) async-start(), calls=%async_computation.12 | async-start | bytes 1310720 | tf_op jit(solution)/shard_map/all_gather | solution.py:611
  99.4 213.9 %all-gather.13.cloned.1.call-start = ((), (), s32[]{:S(2)}) async-start(), calls=%async_computation.13 | async-start | bytes 9437184 | tf_op jit(solution)/shard_map/all_gather | solution.py:725
  143.5 83.7 %collective-permute-start.14 = (bf16[4,1024,512]{2,1,0:T(8,128)(2,1)}, bf16[4,1024,512]{2,1,0:T(8,128)(2,1)}, u32[]{:S(2)}, u32[]{:S(2)}) collective-permute-start(bf16[4,1024,512]{2,1,0:T(8,128)(2,1)} %pad_maximum_fusion.2.mine_ref), channel_id=1, source_target_pairs={{0,4},{4,0},{8,12},{12,8},{16,20},{20,16},{24,28},{28,24},{1,5},{5... | collective-permute-start | bytes 12582920 | tf_op jit(solution)/shard_map/ppermute | solution.py:607
  182.5 65.2 %collective-permute-start.4 = (bf16[4,1024,512]{2,1,0:T(8,128)(2,1)}, bf16[4,1024,512]{2,1,0:T(8,128)(2,1)}, u32[]{:S(2)}, u32[]{:S(2)}) collective-permute-start(bf16[4,1024,512]{2,1,0:T(8,128)(2,1)} %pad_maximum_fusion.mine_ref), channel_id=1, source_target_pairs={{0,4},{4,0},{8,12},{12,8},{16,20},{20,16},{24,28},{28,24},{1,5},{5... | collective-permute-start | bytes 12582920 | tf_op jit(solution)/shard_map/ppermute | solution.py:607
  309.5 63.5 %all-to-all-start.1 = ((bf16[4,640,512]{2,1,0:T(8,128)(2,1)}), bf16[4,640,512]{2,1,0:T(8,128)(2,1)S(1)}, u32[]{:S(2)}, u32[]{:S(2)}) async-start(bf16[4,640,512]{2,1,0:T(8,128)(2,1)} %key.1), calls=%async_computation.1 | async-start | bytes 5242880 | tf_op jit(solution)/shard_map/all_to_all | solution.py:584
  313.2 266.3 %all-gather.15.cloned.1.call-start = ((), (), s32[]{:S(2)}) async-start(), calls=%async_computation.14 | async-start | bytes 9437184 | tf_op jit(solution)/shard_map/all_gather | solution.py:727
  373.0 87.1 %collective-permute-start.19 = (bf16[4,512,1024]{2,1,0:T(8,128)(2,1)}, bf16[4,512,1024]{2,1,0:T(8,128)(2,1)}, u32[]{:S(2)}, u32[]{:S(2)}) collective-permute-start(bf16[4,512,1024]{2,1,0:T(8,128)(2,1)} %pad_maximum_fusion.3.mine_ref), channel_id=1, source_target_pairs={{0,4},{4,0},{8,12},{12,8},{16,20},{20,16},{24,28},{28,24},{1,5},{5... | collective-permute-start | bytes 12582920 | tf_op jit(solution)/shard_map/ppermute | solution.py:607
  428.6 950.3 %reduce-scatter.7.cloned.1.call-start = ((), (), s32[]{:S(2)}) async-start(), calls=%async_computation.15 | async-start | bytes 9437184 | tf_op jit(solution)/shard_map/reduce_scatter | solution.py:775
  587.8 68.8 %collective-permute-start.21 = (bf16[320,2048]{1,0:T(8,128)(2,1)S(1)}, bf16[320,2048]{1,0:T(8,128)(2,1)S(1)}, u32[]{:S(2)}, u32[]{:S(2)}) collective-permute-start(bf16[320,2048]{1,0:T(8,128)(2,1)S(1)} %slice.458), channel_id=1, source_target_pairs={{0,1},{1,0},{2,3},{3,2},{4,5},{5,4},{6,7},{7,6},{8,9},{9,8},{10,11... | collective-permute-start | bytes 3932168 | tf_op jit(solution)/shard_map/ppermute | solution.py:542
  714.0 76.6 %collective-permute-start.32 = (bf16[640,2048]{1,0:T(8,128)(2,1)}, bf16[640,2048]{1,0:T(8,128)(2,1)S(1)}, u32[]{:S(2)}, u32[]{:S(2)}) collective-permute-start(bf16[640,2048]{1,0:T(8,128)(2,1)} %get-tuple-element.75), channel_id=1, source_target_pairs={{0,2},{1,3},{2,0},{3,1},{4,6},{5,7},{6,4},{7,5},{8,10},{9,11},{10,... | collective-permute-start | bytes 7864328 | tf_op jit(solution)/shard_map/ppermute | solution.py:542
  788.1 140.2 %collective-permute-start.31 = (bf16[320,2048]{1,0:T(8,128)(2,1)}, bf16[320,2048]{1,0:T(8,128)(2,1)S(1)}, u32[]{:S(2)}, u32[]{:S(2)}) collective-permute-start(bf16[320,2048]{1,0:T(8,128)(2,1)} %slice.469), channel_id=1, source_target_pairs={{0,1},{1,0},{2,3},{3,2},{4,5},{5,4},{6,7},{7,6},{8,9},{9,8},{10,11... | collective-permute-start | bytes 3932168 | tf_op jit(solution)/shard_map/ppermute | solution.py:542
  812.9 115.5 %collective-permute-start.39 = (bf16[320,2048]{1,0:T(8,128)(2,1)}, bf16[320,2048]{1,0:T(8,128)(2,1)S(1)}, u32[]{:S(2)}, u32[]{:S(2)}) collective-permute-start(bf16[320,2048]{1,0:T(8,128)(2,1)} %slice.474), channel_id=1, source_target_pairs={{0,2},{1,3},{2,0},{3,1},{4,6},{5,7},{6,4},{7,5},{8,10},{9,11},{10,... | collective-permute-start | bytes 3932168 | tf_op jit(solution)/shard_map/ppermute | solution.py:542
  957.5 421.4 %reduce-scatter.9.cloned.1.call-start = ((), (), s32[]{:S(2)}) async-start(), calls=%async_computation.16 | async-start | bytes 9437184 | tf_op jit(solution)/shard_map/reduce_scatter | solution.py:796
  1079.3 364.5 %reduce-scatter.17.cloned.1.call-start = ((), (), s32[]{:S(2)}) async-start(), calls=%async_computation.20 | async-start | bytes 1310720 | tf_op jit(solution)/shard_map/reduce_scatter | solution.py:641
  1090.3 103.2 %collective-permute-start.70 = (bf16[4,512,1024]{2,1,0:T(8,128)(2,1)}, bf16[4,512,1024]{2,1,0:T(8,128)(2,1)}, u32[]{:S(2)}, u32[]{:S(2)}) collective-permute-start(bf16[4,512,1024]{2,1,0:T(8,128)(2,1)} %get-tuple-element.109), channel_id=1, source_target_pairs={{0,4},{4,0},{8,12},{12,8},{16,20},{20,16},{24,28},{28,24},{1,5},{5... | collective-permute-start | bytes 12582920 | tf_op jit(solution)/shard_map/ppermute | solution.py:607
  1152.7 89.6 %collective-permute-start.49 = (bf16[4,1024,512]{2,1,0:T(8,128)(2,1)}, bf16[4,1024,512]{2,1,0:T(8,128)(2,1)}, u32[]{:S(2)}, u32[]{:S(2)}) collective-permute-start(bf16[4,1024,512]{2,1,0:T(8,128)(2,1)} %get-tuple-element.88), channel_id=1, source_target_pairs={{0,4},{4,0},{8,12},{12,8},{16,20},{20,16},{24,28},{28,24},{1,5},{5... | collective-permute-start | bytes 12582920 | tf_op jit(solution)/shard_map/ppermute | solution.py:607
  1166.9 82.4 %collective-permute-start.50 = (bf16[4,1024,512]{2,1,0:T(8,128)(2,1)}, bf16[4,1024,512]{2,1,0:T(8,128)(2,1)}, u32[]{:S(2)}, u32[]{:S(2)}) collective-permute-start(bf16[4,1024,512]{2,1,0:T(8,128)(2,1)} %get-tuple-element.90), channel_id=1, source_target_pairs={{0,4},{4,0},{8,12},{12,8},{16,20},{20,16},{24,28},{28,24},{1,5},{5... | collective-permute-start | bytes 12582920 | tf_op jit(solution)/shard_map/ppermute | solution.py:607
  1193.4 61.4 %collective-permute-start.51 = (bf16[4,1024,512]{2,1,0:T(8,128)(2,1)}, bf16[4,1024,512]{2,1,0:T(8,128)(2,1)}, u32[]{:S(2)}, u32[]{:S(2)}) collective-permute-start(bf16[4,1024,512]{2,1,0:T(8,128)(2,1)} %get-tuple-element.92), channel_id=1, source_target_pairs={{0,4},{4,0},{8,12},{12,8},{16,20},{20,16},{24,28},{28,24},{1,5},{5... | collective-permute-start | bytes 12582920 | tf_op jit(solution)/shard_map/ppermute | solution.py:607
  1242.3 203.3 %reduce-scatter.15.cloned.1.call-start = ((), (), s32[]{:S(2)}) async-start(), calls=%async_computation.19 | async-start | bytes 1310720 | tf_op jit(solution)/shard_map/reduce_scatter | solution.py:641
  1295.3 155.1 %reduce-scatter.13.cloned.1.call-start = ((), (), s32[]{:S(2)}) async-start(), calls=%async_computation.18 | async-start | bytes 1310720 | tf_op jit(solution)/shard_map/reduce_scatter | solution.py:641
  1341.0 109.4 %reduce-scatter.11.cloned.1.call-start = ((), (), s32[]{:S(2)}) async-start(), calls=%async_computation.17 | async-start | bytes 1310720 | tf_op jit(solution)/shard_map/reduce_scatter | solution.py:641
  1349.0 73.6 %collective-permute-start.85 = (f32[8,48,128]{2,1,0:T(8,128)S(1)}, f32[8,48,128]{2,1,0:T(8,128)S(1)}, u32[]{:S(2)}, u32[]{:S(2)}) collective-permute-start(f32[8,48,128]{2,1,0:T(8,128)S(1)} %add.265), channel_id=1, source_target_pairs={{0,8},{4,12},{8,0},{12,4},{16,24},{20,28},{24,16},{28,20},{1,9},{5... | collective-permute-start | bytes 589832 | tf_op jit(solution)/shard_map/ppermute | solution.py:578
  (143 other events, 3143.7 us)
Sparse Core Ops, SparseCore 0:
  10.1 30.6 all-gather.16
  43.0 27.3 all-gather.18
  72.0 27.3 all-gather.8
  100.8 29.1 all-gather.10
  131.5 81.3 all-gather.12
  315.3 83.9 all-gather.14
  928.5 89.7 reduce-scatter.6
  1079.4 89.5 reduce-scatter.8
  1242.4 27.2 reduce-scatter.16
  1295.4 27.3 reduce-scatter.14
  1341.1 31.6 reduce-scatter.12
  1379.1 26.5 reduce-scatter.10
